TPU v7x, 32 devices: a whole 2x2x4 slice. The times are simulated.
32 devices in a mesh: seq: 8 (over z, y), head: 4 (over x, core).
Axes of the slice: x: 2, y: 2, z: 4, core: 2. Of those that a mesh axis runs over, the one named last changes fastest.
Arguments:
- x_raw: bfloat16 [8192, 5120], P('seq', 'head'), may hold values from -6 to 6
- bc_raw: bfloat16 [8192, 256], P('seq'), may hold values from -6 to 6
- z_gate: bfloat16 [8192, 5120], P('seq', 'head'), may hold values from -6 to 6
- dt_raw: float32 [80, 8192], P('head', 'seq'), may hold values from -5.5 to 2.5
- a_log: float32 [80], P('head'), may hold values from -12 to -2
- d_skip: float32 [80], P('head'), may hold values from 0.5 to 1.5
- conv_x: float32 [4, 5120], P(None, 'head'), may hold values from -3 to 3
- conv_bc: float32 [4, 256], replicated, may hold values from -3 to 3
- norm_gain: float32 [5120], P('head'), may hold values from 0.1 to 1.9
- w_out: bfloat16 [5120, 2560], P('head'), may hold values from -0.125 to 0.125
Outputs:
- layer_out: bfloat16 [8192, 2560], P('seq', 'head')
All inputs are finite; a program needn't handle non-finite values.
Results may differ from a plain program's by a relative error of at most 0.015.
Values may be sent and summed in bfloat16 or wider, within the bound.
A program may use at most 128 MiB of HBM per device.

v0:
```python
import jax
import jax.numpy as jnp
from jax import lax
from jax.sharding import PartitionSpec as P

H = 80
P_SIZE = 64
N = 128
Q = 256
CONV = 4


norm_floor = 0.5


def passed_along(value, axis, steps):
    count = lax.axis_size(axis)
    initial, last = (max(0, -steps), min(count, count - steps))
    return lax.ppermute(value, axis, [(source, source + steps) for source in range(initial, last)])


def conv_with(before, raw_rows, taps):
    length = raw_rows.shape[0]
    padded = jnp.concatenate([before, raw_rows], axis=0)
    total = jnp.zeros(raw_rows.shape, jnp.float32)
    for number in range(CONV):
        total = total + padded[number : number + length].astype(jnp.float32) * taps[number][None, :]
    return jax.nn.silu(total).astype(jnp.bfloat16)


def local(x_raw, bc_raw, z_gate, dt_raw, a_log, d_skip, conv_x, conv_bc, norm_gain, w_out):
    length = x_raw.shape[0]
    head_count = a_log.shape[0]
    block_count = length // Q
    width_x = x_raw.shape[1]
    rim_rows = jnp.concatenate(
        [x_raw[length - (CONV - 1) :], bc_raw[length - (CONV - 1) :]], axis=1
    )
    before = passed_along(rim_rows, "seq", 1)
    x_conv = conv_with(before[:, :width_x], x_raw, conv_x)
    bc_conv = conv_with(before[:, width_x:], bc_raw, conv_bc)
    x_heads = x_conv.reshape(block_count, Q, head_count, P_SIZE)
    b_part = bc_conv[:, :N].reshape(block_count, Q, N)
    c_part = bc_conv[:, N:].reshape(block_count, Q, N)
    step_sizes = jax.nn.softplus(dt_raw)
    log_rates = -jnp.exp(a_log)[:, None] * step_sizes
    step_blocks = step_sizes.reshape(head_count, block_count, Q)
    cumulative = jnp.cumsum(log_rates.reshape(head_count, block_count, Q), axis=2)
    scores = jnp.einsum("ctn,csn->cts", c_part, b_part, preferred_element_type=jnp.float32)
    causal = jnp.tril(jnp.ones((Q, Q), bool))
    log_gaps = cumulative[:, :, :, None] - cumulative[:, :, None, :]
    decays = jnp.where(
        causal[None, None], jnp.exp(jnp.where(causal[None, None], log_gaps, 0.0)), 0.0
    )
    weights = (scores[None] * decays * step_blocks[:, :, None, :]).astype(jnp.bfloat16)
    inner_out = jnp.einsum("hcts,cshp->cthp", weights, x_heads, preferred_element_type=jnp.float32)
    tail_decay = jnp.exp(cumulative[:, :, -1:] - cumulative) * step_blocks
    weighted_b = (b_part.astype(jnp.float32)[None] * tail_decay[:, :, :, None]).astype(jnp.bfloat16)
    local_states = jnp.einsum(
        "hcsn,cshp->hcpn", weighted_b, x_heads, preferred_element_type=jnp.float32
    )
    block_logs = cumulative[:, :, -1]
    running = jnp.zeros((head_count, P_SIZE, N), jnp.float32)
    running_log = jnp.zeros((head_count,), jnp.float32)
    prefix_states = []
    prefix_logs = []
    for number in range(block_count):
        prefix_states.append(running)
        prefix_logs.append(running_log)
        running = jnp.exp(block_logs[:, number])[:, None, None] * running + local_states[:, number]
        running_log = running_log + block_logs[:, number]
    zero_state = jnp.zeros((head_count, P_SIZE, N), jnp.float32)
    all_logs = lax.all_gather(running_log[None], "seq", axis=0, tiled=True)
    inclusive = jnp.cumsum(all_logs, axis=0)
    own_index = lax.axis_index("seq")
    own_inclusive = lax.dynamic_index_in_dim(inclusive, own_index, 0, keepdims=False)
    before_own = own_inclusive - running_log
    piece = lax.all_gather(running[None].astype(jnp.bfloat16), "seq", axis=0, tiled=True).astype(
        jnp.float32
    )
    count = piece.shape[0]
    positions = jnp.arange(count, dtype=jnp.int32)
    earlier = (positions < own_index)[:, None]
    exponent = jnp.where(earlier, before_own[None, :] - inclusive, 0.0)
    factors = jnp.where(earlier, jnp.exp(exponent), 0.0)
    entering = zero_state + jnp.einsum(
        "kh,khpn->hpn", factors, piece, precision=lax.Precision.HIGHEST
    )
    prefix_stack = jnp.stack(prefix_states, axis=1)
    prefix_log_stack = jnp.stack(prefix_logs, axis=1)
    block_entering = prefix_stack + jnp.exp(prefix_log_stack)[:, :, None, None] * entering[:, None]
    outer_out = (
        jnp.einsum(
            "ctn,hcpn->cthp",
            c_part.astype(jnp.float32),
            block_entering,
            precision=lax.Precision.HIGHEST,
        )
        * jnp.exp(cumulative).transpose(1, 2, 0)[:, :, :, None]
    )
    mixed = inner_out + outer_out + d_skip[None, None, :, None] * x_heads.astype(jnp.float32)
    mixed = mixed.reshape(length, width_x)
    gated = mixed * jax.nn.silu(z_gate.astype(jnp.float32))
    own_squares = jnp.sum(gated * gated, axis=1)
    unit = (gated * norm_gain[None, :]).astype(jnp.bfloat16)
    group_part = jnp.dot(unit, w_out, preferred_element_type=jnp.float32).astype(jnp.bfloat16)
    total_squares = lax.psum(own_squares, "head")
    row_scale = lax.rsqrt(total_squares / (H * P_SIZE) + norm_floor)
    summed = lax.psum_scatter(group_part, "head", scatter_dimension=1, tiled=True).astype(
        jnp.float32
    )
    return (summed * row_scale[:, None]).astype(jnp.bfloat16)


def solution(mesh):
    in_specs = (
        P("seq", "head"),
        P("seq", None),
        P("seq", "head"),
        P("head", "seq"),
        P("head"),
        P("head"),
        P(None, "head"),
        P(),
        P("head"),
        P("head", None),
    )
    out_specs = P("seq", "head")
    return jax.shard_map(local, mesh=mesh, in_specs=in_specs, out_specs=out_specs, check_vma=False)
```

profile of v0, /device:TPU:25, one launch (start us, length us, event | category | flops | bytes accessed | tf_op | source)
XLA Modules:
  0.0 205.3 jit_solution(13404612665055143535)
XLA Ops:
  6.5 0.8 slice.99
  7.3 0.7 slice.98
  8.0 1.0 copy.43
  9.0 3.1 %collective-permute-start = (bf16[3,1536]{0,1:T(8,128)(2,1)}, bf16[3,1536]{0,1:T(8,128)(2,1)S(1)}, u32[]{:S(2)}, u32[]{:S(2)}) collective-permute-start(bf16[3,1536]{0,1:T(8,128)(2,1)} %copy.43), channel_id=1, source_target_pairs={{0,4},{4,8},{8,12},{12,16},{16,20},{20,24},{24,28},{1,5},{5,9},{9,... | collective-permute-start | bytes 27656 | tf_op jit(solution)/shard_map/ppermute | solution.py:19
  12.2 0.7 exponential_negate_fusion
  12.8 1.0 broadcast_multiply_fusion
  13.8 0.1 reshape.239
  13.9 2.3 %reduce-window.6 = f32[20,4,2,128]{3,0,1,2:T(8,128)S(1)} reduce-window(f32[20,4,2,128]{3,0,1,2:T(8,128)S(1)} %copy.47, f32[]{:T(128)} %constant.21.clone.1), window={size=1x1x1x128 pad=0_0x0_0x0_0x127_0}, to_apply=%region_0.1 | reduce-window | flops 2600960 | bytes 163844 | tf_op jit(solution)/shard_map/reduce-window
  16.2 0.2 slice_reduce_fusion
  16.4 0.1 broadcast_add_fusion
  16.5 0.1 copy.48
  16.6 0.1 reduce_window_sum.38
  16.7 0.1 slice.143
  16.8 0.1 copy.53
  16.9 0.6 fusion.45
  17.5 0.1 copy.54
  17.6 1.4 fusion.44
  19.1 0.7 exponential_bitcast_fusion
  19.8 1.5 slice_reduce_fusion.4
  21.4 3.0 %copy.44 = bf16[1024,1280]{0,1:T(8,128)(2,1)S(1)} copy(bf16[1024,1280]{1,0:T(8,128)(2,1)} %param.10) | data formatting | bytes 5242880 | tf_op args[0]
  24.4 0.7 slice.134
  25.1 0.9 copy.46
  26.0 0.0 copy-done.9
  26.0 1.4 multiply_convert_fusion.10
  27.4 0.8 convert_element_type.85
  28.2 1.0 slice.129
  29.2 6.9 %multiply_convert_fusion.5 = bf16[1024,1280]{0,1:T(8,128)(2,1)} fusion(bf16[1024,1280]{0,1:T(8,128)(2,1)S(1)} %copy.44, bf16[3,1280]{0,1:T(8,128)(2,1)S(1)} %slice.129, f32[1280]{0:T(1024)} %get-tuple-element.7, f32[1280]{0:T(1024)} %get-tuple-element.8, f32[1280]{0:T(1024)} %get-tuple-element.6, f32[1280]{0:T(1024)S(1)} %get-tuple-element.5), kind=kLoop, calls=%fused_computation.23 | loop fusion | flops 32768000 | bytes 5271040 | tf_op jit(solution)/shard_map/convert_element_type | solution.py:28
  36.1 4.4 %reshape.236 = bf16[4,256,20,64]{1,0,3,2:T(4,128)(2,1)S(1)} reshape(bf16[1024,1280]{0,1:T(8,128)(2,1)} %multiply_convert_fusion.5) | data formatting | bytes 5242880 | tf_op jit(solution)/shard_map/reshape | solution.py:42
  40.6 5.5 %fusion.11 = f32[20,4,64,128]{3,2,1,0:T(8,128)S(1)} fusion(f32[20,4,256]{2,1,0:T(4,128)S(1)} %copy-done.15, f32[4,256,128]{2,1,0:T(8,128)} %convert_element_type.85, bf16[4,256,20,64]{1,0,3,2:T(4,128)(2,1)S(1)} %reshape.236), kind=kOutput, calls=%fused_computation.16 | convolution fusion | flops 340787200 | bytes 5849088 | tf_op jit(solution)/shard_map/hcsn,cshp->hcpn/dot_general | solution.py:59
  46.1 1.5 copy-done.1
  47.6 1.0 fusion.33
  48.7 0.0 all-gather.3.cloned.1.call-update
  48.7 0.0 reduce-scatter.4.cloned.1.call-start
  48.7 0.7 copy.51
  49.4 0.6 copy.49
  50.1 0.6 dynamic-slice
  51.3 0.1 bitcast_dynamic-update-slice_fusion
  51.4 12.1 %all-reduce = f32[160]{0:T(256)S(1)} all-reduce(f32[160]{0:T(256)S(1)} %get-tuple-element.9), channel_id=2, replica_groups=mesh['seq'=8,'head'=4] {'seq'}, use_global_device_ids=true, to_apply=%add | all-reduce | flops 160 | bytes 1280
  63.5 0.1 reshape.242
  63.6 0.1 select_bitcast_fusion
  63.7 0.1 copy.63
  63.8 0.7 copy.59
  64.5 3.0 %copy.62 = bf16[1024,1280]{0,1:T(8,128)(2,1)S(1)} copy(bf16[1024,1280]{1,0:T(8,128)(2,1)} %param.12) | data formatting | bytes 5242880 | tf_op args[2]
  67.5 0.5 pad.4.clone
  68.0 0.6 iota_compare_fusion
  68.6 1.3 fusion.47
  69.9 2.8 %bitcast_add_fusion.4 = (f32[20,1,64,128]{3,2,0,1:T(8,128)S(1)}, f32[20,1,64,128]{3,2,0,1:T(8,128)}, f32[20,1,64,128]{3,2,0,1:T(8,128)}) fusion(f32[20,4,64,128]{3,2,1,0:T(8,128)} %copy-done.1, f32[20]{0:T(128)} %get-tuple-element.28, f32[20]{0:T(128)} %get-tuple-element.29, f32[20]{0:T(128)} %get-tuple-element.26), kind=kLoop, calls=%fused_computation.60 | loop fusion | flops 819200 | bytes 3932400 | tf_op jit(solution)/shard_map/add | solution.py:70
  72.7 28.8 %all-gather.3.cloned.1.call-done = bf16[8,20,64,128]{3,2,1,0:T(8,128)(2,1)} async-done(((bf16[1,20,64,128]{3,2,1,0:T(8,128)(2,1)}), bf16[8,20,64,128]{3,2,1,0:T(8,128)(2,1)}) %all-gather.3.cloned.1.call-update) | async-done | bytes 2621456 | tf_op jit(solution)/shard_map/all_gather | solution.py:78
  101.6 5.0 %fusion.23 = f32[20,1,64,128]{3,1,2,0:T(1,128)S(1)} fusion(f32[8,20,1,1]{0,2,3,1:T(1,128)S(1)} %copy.63, bf16[8,20,64,128]{3,2,1,0:T(8,128)(2,1)} %all-gather.3.cloned.1.call-done), kind=kOutput, calls=%fused_computation.38 | convolution fusion | flops 15728640 | bytes 3277440 | tf_op jit(solution)/shard_map/kh,khpn->hpn/dot_general | solution.py:86
  106.6 3.6 %fusion.17 = f32[4,256,20,64]{1,3,2,0:T(8,128)S(1)} fusion(bf16[4,256,128,1]{2,1,3,0:T(8,128)(2,1)S(1)} %bitcast.95, f32[20,1,64,128]{3,2,0,1:T(8,128)S(1)} %get-tuple-element.12, f32[20,1,64,128]{3,2,0,1:T(8,128)} %get-tuple-element.13, f32[20,1,64,128]{3,2,0,1:T(8,128)} %get-tuple-element.14, f32[4]{0:T(128)} %pad.4.clone, ...), kind=kOutput, calls=%fused_computation.32 | convolution fusion | flops 2016542720 | bytes 8126800 | tf_op jit(solution)/shard_map/ctn,hcpn->cthp/dot_general | solution.py:93
  110.2 7.6 %fusion.12 = f32[4,256,20,64]{1,3,2,0:T(8,128)S(1)} fusion(f32[4,256,20,64]{1,3,2,0:T(8,128)S(1)} %fusion.17, f32[20]{0:T(128)S(1)} %copy-done.23, f32[4,256,20]{1,2,0:T(8,128)S(1)} %copy-done.14, f32[20,4,256]{2,0,1:T(8,128)S(1)} %copy-done.12, f32[20,4,256]{2,0,1:T(8,128)S(1)} %copy-done.13, f32[4,256,256]{2,1,0:T(8,128)S(1)} %copy-done.4, ...), kind=kOutput, calls=%fused_computation.18 | convolution fusion | flops 709099520 | bytes 14467152 | tf_op jit(solution)/shard_map/hcts,cshp->cthp/dot_general | solution.py:56
  117.8 0.0 slice-start
  117.9 3.9 %copy.61 = f32[4,256,20,64]{1,0,3,2:T(4,128)S(1)} copy(f32[4,256,20,64]{1,3,2,0:T(8,128)S(1)} %fusion.12) | data formatting | bytes 10485760 | tf_op jit(solution)/shard_map/add | solution.py:101
  121.8 0.0 slice-start.1
  121.8 1.3 copy.72
  123.1 2.3 %copy-done = f32[160,8,4,256]{3,1,2,0:T(8,128)} copy-done((f32[160,8,4,256]{3,1,2,0:T(8,128)}, f32[160,8,4,256]{3,1,2,0:T(8,128)S(1)}, u32[]{:S(2)}) %copy-start) | copy-done | bytes 5242904
  125.4 9.9 %convolution_convert_fusion = bf16[1024,2560]{1,0:T(8,128)(2,1)} fusion(bf16[1280,2560]{1,0:T(8,128)(2,1)S(1)} %bitcast.108, f32[1280]{0:T(1024)S(1)} %copy-done.22, f32[1024,1280]{0,1:T(8,128)S(1)} %bitcast.90, bf16[1024,1280]{0,1:T(8,128)(2,1)S(1)} %copy.62), kind=kOutput, calls=%fused_computation.11 | convolution fusion | flops 6723993600 | bytes 19665920 | tf_op jit(solution)/shard_map/dot_general | solution.py:106
  135.3 7.9 %copy.67 = bf16[1024,2560]{0,1:T(8,128)(2,1)} copy(bf16[1024,2560]{1,0:T(8,128)(2,1)} %convolution_convert_fusion) | data formatting | bytes 10485760
  143.3 0.0 reduce-scatter.4.cloned.1.call-update
  143.3 4.2 %multiply_reduce_fusion = f32[1024]{0:T(1024)S(1)} fusion(f32[1024,1280]{0,1:T(8,128)} %bitcast.91, bf16[1024,1280]{0,1:T(8,128)(2,1)S(1)} %copy.62), kind=kLoop, calls=%fused_computation.19 | loop fusion | flops 10484736 | bytes 7868416 | tf_op jit(solution)/shard_map/reduce_sum | solution.py:104
  147.5 6.4 %psum.7 = f32[1024]{0:T(1024)S(1)} all-reduce(f32[1024]{0:T(1024)S(1)} %multiply_reduce_fusion), channel_id=1, replica_groups=mesh['seq'=8,'head'=4] {'head'}, use_global_device_ids=true, to_apply=%region_5.6 | all-reduce | flops 1024 | bytes 8192 | tf_op jit(solution)/shard_map/psum | solution.py:107
  153.9 41.4 %reduce-scatter.4.cloned.1.call-done = bf16[640,1024]{1,0:T(8,128)(2,1)} async-done(((bf16[2560,1024]{1,0:T(8,128)(2,1)}), bf16[640,1024]{1,0:T(8,128)(2,1)}) %reduce-scatter.4.cloned.1.call-update) | async-done | bytes 1310736
  195.4 1.7 copy.68
  197.1 1.3 multiply_convert_fusion.7
  (65 shorter events, 0.3 us)
Async XLA Ops:
  6.5 19.4 %copy-start.9 = (bf16[1024,256]{1,0:T(8,128)(2,1)S(1)}, bf16[1024,256]{1,0:T(8,128)(2,1)}, u32[]{:S(2)}) copy-start(bf16[1024,256]{1,0:T(8,128)(2,1)} %param.11) | copy-start | bytes 1572868
  6.5 95.0 %all-gather.3.cloned.1.call-start = ((), (), s32[]{:S(2)}) async-start(), calls=%async_computation.1 | async-start | bytes 2949120 | tf_op jit(solution)/shard_map/all_gather | solution.py:78
  9.0 15.3 %collective-permute-start = (bf16[3,1536]{0,1:T(8,128)(2,1)}, bf16[3,1536]{0,1:T(8,128)(2,1)S(1)}, u32[]{:S(2)}, u32[]{:S(2)}) collective-permute-start(bf16[3,1536]{0,1:T(8,128)(2,1)} %copy.43), channel_id=1, source_target_pairs={{0,4},{4,8},{8,12},{12,16},{16,20},{20,24},{24,28},{1,5},{5,9},{9,... | collective-permute-start | bytes 27656 | tf_op jit(solution)/shard_map/ppermute | solution.py:19
  16.7 3.1 %copy-start.5 = (f32[20,4,256]{2,1,0:T(4,128)}, f32[20,4,256]{2,1,0:T(4,128)S(1)}, u32[]{:S(2)}) copy-start(f32[20,4,256]{2,1,0:T(4,128)S(1)} %reduce_window_sum.38) | copy-start | bytes 245764
  19.1 0.7 copy-start.7
  24.4 1.6 copy-start.10
  36.1 4.4 %copy-start.15 = (f32[20,4,256]{2,1,0:T(4,128)S(1)}, f32[20,4,256]{2,1,0:T(4,128)}, u32[]{:S(2)}) copy-start(f32[20,4,256]{2,1,0:T(4,128)} %get-tuple-element.20) | copy-start | bytes 245764
  40.5 5.6 %copy-start.2 = (bf16[4,256,20,64]{1,0,3,2:T(4,128)(2,1)}, bf16[4,256,20,64]{1,0,3,2:T(4,128)(2,1)S(1)}, u32[]{:S(2)}) copy-start(bf16[4,256,20,64]{1,0,3,2:T(4,128)(2,1)S(1)} %reshape.236) | copy-start | bytes 7864324
  40.5 7.1 %copy-start.17 = (f32[20]{0:T(128)S(1)}, f32[20]{0:T(128)}, u32[]{:S(2)}) copy-start(f32[20]{0:T(128)} %get-tuple-element.26) | copy-start | bytes 244
  40.5 7.1 %copy-start.18 = (f32[20]{0:T(128)S(1)}, f32[20]{0:T(128)}, u32[]{:S(2)}) copy-start(f32[20]{0:T(128)} %get-tuple-element.28) | copy-start | bytes 244
  40.5 7.1 %copy-start.19 = (f32[20]{0:T(128)S(1)}, f32[20]{0:T(128)}, u32[]{:S(2)}) copy-start(f32[20]{0:T(128)} %get-tuple-element.29) | copy-start | bytes 244
  40.6 7.1 %copy-start.20 = (f32[20]{0:T(128)S(1)}, f32[20]{0:T(128)}, u32[]{:S(2)}) copy-start(f32[20]{0:T(128)} %get-tuple-element.27) | copy-start | bytes 244
  40.6 8.2 %copy-start.8 = (f32[20,4,256]{2,1,0:T(4,128)S(1)}, f32[20,4,256]{2,1,0:T(4,128)}, u32[]{:S(2)}) copy-start(f32[20,4,256]{2,1,0:T(4,128)} %copy-done.7) | copy-start | bytes 245764
  40.6 8.8 %copy-start.6 = (f32[20,4,256]{2,1,0:T(4,128)S(1)}, f32[20,4,256]{2,1,0:T(4,128)}, u32[]{:S(2)}) copy-start(f32[20,4,256]{2,1,0:T(4,128)} %copy-done.5) | copy-start | bytes 245764
  40.6 9.5 %copy-start.24 = (u32[32]{0:T(128)S(1)}, u32[32]{0:T(128)}, u32[]{:S(2)}) copy-start(u32[32]{0:T(128)} %constant.41) | copy-start | bytes 388
  40.6 23.2 %copy-start.11 = (f32[4,256,20]{1,0,2:T(4,128)S(1)}, f32[4,256,20]{1,0,2:T(4,128)}, u32[]{:S(2)}) copy-start(f32[4,256,20]{1,0,2:T(4,128)} %get-tuple-element.19) | copy-start | bytes 245764
  46.1 1.5 copy-start.1
  46.1 21.9 %copy-start.21 = (f32[20,1]{0,1:T(1,128)S(1)}, f32[20,1]{0,1:T(1,128)}, u32[]{:S(2)}) copy-start(f32[20,1]{0,1:T(1,128)} %get-tuple-element.25) | copy-start | bytes 244
  48.7 146.7 %reduce-scatter.4.cloned.1.call-start = ((), (), s32[]{:S(2)}) async-start(), calls=%async_computation.2 | async-start | bytes 6553600
  101.5 8.6 %copy-start.3 = (bf16[4,256,20,64]{1,0,3,2:T(4,128)(2,1)S(1)}, bf16[4,256,20,64]{1,0,3,2:T(4,128)(2,1)}, u32[]{:S(2)}) copy-start(bf16[4,256,20,64]{1,0,3,2:T(4,128)(2,1)} %copy-done.2) | copy-start | bytes 7864324
  101.5 8.6 %copy-start.4 = (f32[4,256,256]{2,1,0:T(8,128)S(1)}, f32[4,256,256]{2,1,0:T(8,128)}, u32[]{:S(2)}) copy-start(f32[4,256,256]{2,1,0:T(8,128)} %fusion.47) | copy-start | bytes 3145732
  101.5 8.6 %copy-start.12 = (f32[20,4,256]{2,0,1:T(8,128)S(1)}, f32[20,4,256]{2,0,1:T(8,128)}, u32[]{:S(2)}) copy-start(f32[20,4,256]{2,0,1:T(8,128)} %copy.51) | copy-start | bytes 245764
  101.5 8.7 %copy-start.13 = (f32[20,4,256]{2,0,1:T(8,128)S(1)}, f32[20,4,256]{2,0,1:T(8,128)}, u32[]{:S(2)}) copy-start(f32[20,4,256]{2,0,1:T(8,128)} %copy.49) | copy-start | bytes 245764
  101.5 8.7 %copy-start.14 = (f32[4,256,20]{1,2,0:T(8,128)S(1)}, f32[4,256,20]{1,2,0:T(8,128)}, u32[]{:S(2)}) copy-start(f32[4,256,20]{1,2,0:T(8,128)} %copy.59) | copy-start | bytes 245764
  101.5 8.7 %copy-start.16 = (pred[256,256]{1,0:T(8,128)(4,1)S(1)}, pred[256,256]{1,0:T(8,128)(4,1)}, u32[]{:S(2)}) copy-start(pred[256,256]{1,0:T(8,128)(4,1)} %iota_compare_fusion) | copy-start | bytes 196612
  101.6 8.7 %copy-start.23 = (f32[20]{0:T(128)S(1)}, f32[20]{0:T(128)}, u32[]{:S(2)}) copy-start(f32[20]{0:T(128)} %param.15) | copy-start | bytes 244
  117.8 7.6 %slice-start = ((s8[6553600]{0:T(1024)(128)(4,1)}), s8[2359296]{0:T(1024)(128)(4,1)S(1)}, s32[]{:S(2)}) async-start(s8[6553600]{0:T(1024)(128)(4,1)} %bitcast.107), calls=%async_computation.3 | async-start | bytes 4718592
  121.8 3.7 %slice-start.1 = ((s8[6553600]{0:T(1024)(128)(4,1)}), s8[4194304]{0:T(1024)(128)(4,1)S(1)}, s32[]{:S(2)}) async-start(s8[6553600]{0:T(1024)(128)(4,1)} %bitcast.107), calls=%async_computation.4 | async-start | bytes 8388608
  121.8 3.6 %copy-start.22 = (f32[1280]{0:T(1024)S(1)}, f32[1280]{0:T(1024)}, u32[]{:S(2)}) copy-start(f32[1280]{0:T(1024)} %param.18) | copy-start | bytes 15364
  123.1 2.3 %copy-start = (f32[160,8,4,256]{3,1,2,0:T(8,128)}, f32[160,8,4,256]{3,1,2,0:T(8,128)S(1)}, u32[]{:S(2)}) copy-start(f32[160,8,4,256]{3,1,2,0:T(8,128)S(1)} %copy.72) | copy-start | bytes 15728644
Sparse Core Ops, SparseCore 0:
  48.8 52.6 all-gather.2
  143.4 51.9 reduce-scatter.3
where the time goes:
time: 208 us; the launch traced here: 205 us
  waiting for transfers between devices  70.3 us (34%)
  local copies, waits for them, and re-layouts  41.2 us (20%)
  matrix products  32.8 us (16%)
  other arithmetic  24.8 us (12%)
  blocking collectives  18.5 us (9%)
  between operations  14.5 us (7%)
  starting transfers between devices  3.18 us (2%)
    unnamed x3, waiting for transfers between devices  41.4 us
    all_gather x1, waiting for transfers between devices, local(): lax.all_gather(running[None].astype(jnp.bfloat16), 'seq', axis=0, tiled=T...  28.8 us
    unnamed x61, local copies, waits for them, and re-layouts  21.4 us
    unnamed x1, blocking collectives  12.1 us
    dot_general x1, matrix products, local(): jnp.dot(unit, w_out, preferred_element_type=jnp.float32)  9.89 us
    convert_element_type x2, other arithmetic, conv_with(): return jax.nn.silu(total).astype(jnp.bfloat16)  8.26 us
    dot_general x1, matrix products, local(): jnp.einsum('hcts,cshp->cthp', weights, x_heads, preferred_element_type=jn...  7.62 us
    psum x1, blocking collectives, local(): total_squares = lax.psum(own_squares, 'head')  6.44 us
  transfers between devices with their start and end apart: 3, of which 2 were waited for; matrix products, arithmetic and copies ran while one was open for 13% of the time, Pallas kernels for 0%

commit v1 on v0

v1 whole, which is shorter than its diff:
```python
import functools

import jax
import jax.numpy as jnp
import numpy as np
from jax import lax
from jax.experimental import pallas as pl
from jax.experimental.pallas import tpu as pltpu
from jax.sharding import PartitionSpec as P

P_SIZE = 64
N = 128
Q = 256
CONV = 4
RIM = 16
CHUNK = 256
SLOT = 32

norm_floor = 0.5


def passed_along(value, axis, steps):
    count = lax.axis_size(axis)
    initial, last = (max(0, -steps), min(count, count - steps))
    return lax.ppermute(value, axis, [(source, source + steps) for source in range(initial, last)])


def silu(v):
    return v / (1.0 + jnp.exp(-v))


def dot_t(a, b):
    return lax.dot_general(a, b, (((0,), (0,)), ((), ())), preferred_element_type=jnp.float32)


def conv_rows(padded_ref, taps, cols, rows):
    total = padded_ref[pl.ds(RIM - CONV + 1, rows), cols] * taps[0:1]
    for number in range(1, CONV):
        total = total + padded_ref[pl.ds(RIM - CONV + 1 + number, rows), cols] * taps[number : number + 1]
    return silu(total)


def store_split(ref, at, value, heads):
    high = value.astype(jnp.bfloat16)
    low = (value - high.astype(jnp.float32)).astype(jnp.bfloat16)
    width = value.shape[1]
    ref[0:heads, at : at + width] = high
    ref[SLOT : SLOT + heads, at : at + width] = low


def intra_kernel(
    heads, width,
    x_ref, xprev_ref, bc_ref, bcprev_ref, before_ref, dt_ref, a_ref, d_ref, cx_ref, cbc_ref, spread_ref, tri_ref,
    base_ref, c_ref, fac2_ref, state_ref, log_ref,
    xpad, bcpad, fac, run, plog, bt, masked,
):
    block = pl.program_id(0)

    @pl.when(block == 0)
    def _():
        run[...] = jnp.zeros_like(run)
        plog[...] = jnp.zeros_like(plog)
        fac[...] = jnp.zeros_like(fac)
        xpad[0:RIM, :] = before_ref[:, 0:width].astype(jnp.float32)
        bcpad[0:RIM, :] = before_ref[:, width : width + 2 * N].astype(jnp.float32)

    @pl.when(block > 0)
    def _():
        xpad[0:RIM, :] = xprev_ref[...].astype(jnp.float32)
        bcpad[0:RIM, :] = bcprev_ref[...].astype(jnp.float32)

    xpad[RIM : RIM + Q, :] = x_ref[...].astype(jnp.float32)
    bcpad[RIM : RIM + Q, :] = bc_ref[...].astype(jnp.float32)
    bc = conv_rows(bcpad, cbc_ref[...], slice(None), Q)
    b_part = bc[:, :N].astype(jnp.bfloat16)
    c_part = bc[:, N:].astype(jnp.bfloat16)
    c_ref[...] = c_part
    bt[...] = bc[:, :N].T.astype(jnp.bfloat16)
    scores = lax.dot_general(c_part, b_part, (((1,), (1,)), ((), ())), preferred_element_type=jnp.float32)
    rows_at = lax.broadcasted_iota(jnp.int32, (Q, Q), 0)
    cols_at = lax.broadcasted_iota(jnp.int32, (Q, Q), 1)
    masked[...] = jnp.where(rows_at >= cols_at, scores, 0.0).astype(jnp.bfloat16)

    dt = dt_ref[...]
    step = jnp.maximum(dt, 0.0) + jnp.log1p(jnp.exp(-jnp.abs(dt)))
    rate = -jnp.exp(a_ref[...]) * step
    tri = tri_ref[...]
    cum = jnp.zeros_like(rate)
    rest = rate
    for _ in range(3):
        piece = rest.astype(jnp.bfloat16)
        cum = cum + jnp.dot(piece, tri, preferred_element_type=jnp.float32)
        rest = rest - piece.astype(jnp.float32)
    last = cum[:, Q - 1 : Q]
    mid = 0.5 * last
    store_split(fac, 0, jnp.exp(cum - mid), heads)
    store_split(fac, Q, jnp.exp(mid - cum) * step, heads)
    lane = lax.broadcasted_iota(jnp.int32, (heads, 128), 1)
    scal = jnp.where(lane == 0, last, jnp.where(lane == 1, mid, last - mid))
    store_split(fac, 2 * Q, jnp.exp(scal), heads)
    before_log = plog[...][:, 0:1]
    fac2_ref[...] = jnp.zeros_like(fac2_ref)
    store_split(fac2_ref, 0, jnp.exp(before_log + cum), heads)
    plog[...] = jnp.broadcast_to(before_log + last, plog.shape)
    log_ref[...] = plog[...]

    for col in range(0, width, CHUNK):
        cols = slice(col, col + CHUNK)
        wide = dot_t(fac[...], spread_ref[:, cols])
        xc = conv_rows(xpad, cx_ref[:, cols], cols, Q).astype(jnp.bfloat16).astype(jnp.float32)
        scaled = (xc * wide[Q : 2 * Q]).astype(jnp.bfloat16)
        held = run[:, cols]
        decay = wide[2 * Q : 2 * Q + 1]
        to_mid = wide[2 * Q + 1 : 2 * Q + 2]
        from_mid = wide[2 * Q + 2 : 2 * Q + 3]
        y = jnp.dot(masked[...], scaled, preferred_element_type=jnp.float32)
        y = y + jnp.dot(c_part, (held * to_mid).astype(jnp.bfloat16), preferred_element_type=jnp.float32)
        base_ref[:, cols] = wide[0:Q] * y + d_ref[:, cols] * xc
        added = jnp.dot(bt[...], scaled, preferred_element_type=jnp.float32)
        new = held * decay + from_mid * added
        run[:, cols] = new
        state_ref[:, cols] = new.astype(jnp.bfloat16)


def project_kernel(width, base_ref, z_ref, c_ref, fac2_ref, enter_ref, gain_ref, spread_ref, w_ref, part_ref, sq_ref, unit):
    total = jnp.zeros((Q, 128), jnp.float32)
    for col in range(0, width, CHUNK):
        cols = slice(col, col + CHUNK)
        wide = dot_t(fac2_ref[...], spread_ref[:, cols])
        outer = jnp.dot(c_ref[...], enter_ref[:, cols], preferred_element_type=jnp.float32)
        mixed = base_ref[:, cols] + wide * outer
        gated = mixed * silu(z_ref[:, cols].astype(jnp.float32))
        square = gated * gated
        for part in range(0, CHUNK, 128):
            total = total + square[:, part : part + 128]
        unit[:, cols] = (gated * gain_ref[:, cols]).astype(jnp.bfloat16)
    sq_ref[...] = lax.dot_general(
        jnp.ones((8, 128), jnp.float32), total, (((1,), (1,)), ((), ())),
        precision=lax.Precision.HIGHEST, preferred_element_type=jnp.float32,
    )
    part_ref[...] = jnp.dot(unit[...], w_ref[...], preferred_element_type=jnp.float32).astype(jnp.bfloat16)


def full(shape):
    return pl.BlockSpec(shape, lambda i: (0,) * len(shape))


def local(channels, x_raw, bc_raw, z_gate, dt_raw, a_log, d_skip, conv_x, conv_bc, norm_gain, w_out):
    length, width = x_raw.shape
    heads = a_log.shape[0]
    blocks = length // Q
    depth = w_out.shape[1]
    spread = np.zeros((2 * SLOT, width), np.float32)
    for head in range(heads):
        spread[head, head * P_SIZE : (head + 1) * P_SIZE] = 1.0
        spread[SLOT + head, head * P_SIZE : (head + 1) * P_SIZE] = 1.0
    spread = jnp.asarray(spread, jnp.bfloat16)
    tri = jnp.asarray(np.triu(np.ones((Q, Q), np.float32)), jnp.bfloat16)
    rim_rows = jnp.concatenate([x_raw[length - RIM :], bc_raw[length - RIM :]], axis=1)
    before = passed_along(rim_rows, "seq", 1)
    d_wide = jnp.repeat(d_skip, P_SIZE)[None]
    prev = lambda i: (jnp.maximum(i * (Q // RIM) - 1, 0), 0)
    f32, bf16 = jnp.float32, jnp.bfloat16
    base, c_part, fac2, state, logs = pl.pallas_call(
        functools.partial(intra_kernel, heads, width),
        grid=(blocks,),
        in_specs=[
            pl.BlockSpec((Q, width), lambda i: (i, 0)),
            pl.BlockSpec((RIM, width), prev),
            pl.BlockSpec((Q, 2 * N), lambda i: (i, 0)),
            pl.BlockSpec((RIM, 2 * N), prev),
            full((RIM, width + 2 * N)),
            pl.BlockSpec((heads, Q), lambda i: (0, i)),
            full((heads, 1)),
            full((1, width)),
            full((CONV, width)),
            full((CONV, 2 * N)),
            full((2 * SLOT, width)),
            full((Q, Q)),
        ],
        out_specs=[
            pl.BlockSpec((Q, width), lambda i: (i, 0)),
            pl.BlockSpec((Q, N), lambda i: (i, 0)),
            pl.BlockSpec((2 * SLOT, Q), lambda i: (0, i)),
            full((N, width)),
            full((heads, 128)),
        ],
        out_shape=[
            jax.ShapeDtypeStruct((length, width), f32),
            jax.ShapeDtypeStruct((length, N), bf16),
            jax.ShapeDtypeStruct((2 * SLOT, length), bf16),
            jax.ShapeDtypeStruct((N, width), bf16),
            jax.ShapeDtypeStruct((heads, 128), f32),
        ],
        scratch_shapes=[
            pltpu.VMEM((RIM + Q, width), f32),
            pltpu.VMEM((RIM + Q, 2 * N), f32),
            pltpu.VMEM((2 * SLOT, 2 * Q + 128), bf16),
            pltpu.VMEM((N, width), f32),
            pltpu.VMEM((heads, 128), f32),
            pltpu.VMEM((N, Q), bf16),
            pltpu.VMEM((Q, Q), bf16),
        ],
        compiler_params=pltpu.CompilerParams(dimension_semantics=("arbitrary",)),
    )(x_raw, x_raw, bc_raw, bc_raw, before, dt_raw, a_log[:, None], d_wide, conv_x, conv_bc, spread, tri)

    own_log = logs[:, 0]
    all_logs = lax.all_gather(own_log[None], "seq", axis=0, tiled=True)
    inclusive = jnp.cumsum(all_logs, axis=0)
    own_index = lax.axis_index("seq")
    own_inclusive = lax.dynamic_index_in_dim(inclusive, own_index, 0, keepdims=False)
    before_own = own_inclusive - own_log
    piece = lax.all_gather(state[None], "seq", axis=0, tiled=True).astype(f32)
    positions = jnp.arange(piece.shape[0], dtype=jnp.int32)
    earlier = (positions < own_index)[:, None]
    exponent = jnp.where(earlier, before_own[None, :] - inclusive, 0.0)
    factors = jnp.where(earlier, jnp.exp(exponent), 0.0)
    entering = jnp.sum(piece * jnp.repeat(factors, P_SIZE, axis=1)[:, None, :], axis=0).astype(bf16)

    part, squares = pl.pallas_call(
        functools.partial(project_kernel, width),
        grid=(blocks,),
        in_specs=[
            pl.BlockSpec((Q, width), lambda i: (i, 0)),
            pl.BlockSpec((Q, width), lambda i: (i, 0)),
            pl.BlockSpec((Q, N), lambda i: (i, 0)),
            pl.BlockSpec((2 * SLOT, Q), lambda i: (0, i)),
            full((N, width)),
            full((1, width)),
            full((2 * SLOT, width)),
            full((width, depth)),
        ],
        out_specs=[pl.BlockSpec((Q, depth), lambda i: (i, 0)), pl.BlockSpec((8, Q), lambda i: (0, i))],
        out_shape=[jax.ShapeDtypeStruct((length, depth), bf16), jax.ShapeDtypeStruct((8, length), f32)],
        scratch_shapes=[pltpu.VMEM((Q, width), bf16)],
        compiler_params=pltpu.CompilerParams(dimension_semantics=("arbitrary",), vmem_limit_bytes=60 << 20),
    )(base, z_gate, c_part, fac2, entering, norm_gain[None], spread, w_out)

    row_scale = lax.rsqrt(lax.psum(squares[0], "head") / channels + norm_floor)
    summed = lax.psum_scatter(part, "head", scatter_dimension=1, tiled=True).astype(f32)
    return (summed * row_scale[:, None]).astype(bf16)


def solution(mesh):
    in_specs = (
        P("seq", "head"),
        P("seq", None),
        P("seq", "head"),
        P("head", "seq"),
        P("head"),
        P("head"),
        P(None, "head"),
        P(),
        P("head"),
        P("head", None),
    )

    def whole(x_raw, *rest):
        body = functools.partial(local, x_raw.shape[1])
        return jax.shard_map(
            body, mesh=mesh, in_specs=in_specs, out_specs=P("seq", "head"), check_vma=False
        )(x_raw, *rest)

    return whole
```

time: 208 us -> 174 us (0.84)
  matrix products: 32.8 us -> 0 us
  Pallas kernels: 0 us -> 29.9 us
  local copies, waits for them, and re-layouts: 41.2 us -> 17.7 us
  other arithmetic: 24.8 us -> 4.56 us
  waiting for transfers between devices: 70.3 us -> 82.6 us
    dot_general x6 -> x0, matrix products: 32.8 us -> none  [the longest x1 9.89 us: local(): jnp.dot(unit, w_out, preferred_element_type=jnp.float32)]
    pallas_call x0 -> x2, Pallas kernels: none -> 29.9 us  [the longest x1 16.5 us: local(): pl.pallas_call(functools.partial(project_kernel, width), grid=(blocks,),...]
    unnamed x61 -> x11, local copies, waits for them, and re-layouts: 21.4 us -> 11.1 us
    convert_element_type x5 -> x1, other arithmetic: 11.5 us -> 1.35 us  [local(): return (summed * row_scale[:, None]).astype(bf16)]
    all_gather x1, waiting for transfers between devices: 28.8 us -> 37.6 us  [local(): piece = lax.all_gather(state[None], 'seq', axis=0, tiled=True).astype(f32)]
    reshape x3 -> x0, local copies, waits for them, and re-layouts: 4.46 us -> none  [the longest x1 4.37 us: local(): x_heads = x_conv.reshape(block_count, Q, head_count, P_SIZE)]
    slice x11 -> x4, local copies, waits for them, and re-layouts: 7.47 us -> 3.06 us  [the longest x1 0.82 us: local(): own_log = logs[:, 0]]
    add x1 -> x0, local copies, waits for them, and re-layouts: 3.89 us -> none  [local(): inner_out + outer_out]
  transfers between devices with their start and end apart: 3 -> 3, of which waited for: 2 -> 2; matrix products, arithmetic and copies ran while one was open for 13% -> 4% of each run, Pallas kernels for 0% -> 0%
where the time goes in v1:
time: 174 us; the launch traced here: 171 us
  waiting for transfers between devices  82.6 us (47%)
  Pallas kernels  29.9 us (17%)
  blocking collectives  19.1 us (11%)
  local copies, waits for them, and re-layouts  17.7 us (10%)
  between operations  14 us (8%)
  other arithmetic  4.56 us (3%)
  starting transfers between devices  3.18 us (2%)
    unnamed x3, waiting for transfers between devices  44.9 us
    all_gather x1, waiting for transfers between devices, local(): piece = lax.all_gather(state[None], 'seq', axis=0, tiled=True).astype(f32)  37.6 us
    pallas_call x1, Pallas kernels, local(): pl.pallas_call(functools.partial(project_kernel, width), grid=(blocks,),...  16.5 us
    pallas_call x1, Pallas kernels, local(): pl.pallas_call(functools.partial(intra_kernel, heads, width), grid=(block...  13.3 us
    unnamed x1, blocking collectives  12.7 us
    unnamed x11, local copies, waits for them, and re-layouts  11.1 us
    psum x1, blocking collectives, local(): row_scale = lax.rsqrt(lax.psum(squares[0], 'head') / channels + norm_floor)  6.4 us
  transfers between devices with their start and end apart: 3, of which 2 were waited for; matrix products, arithmetic and copies ran while one was open for 4% of the time, Pallas kernels for 0%

profile of v1, /device:TPU:25, one launch (start us, length us, event | category | flops | bytes accessed | tf_op | source)
XLA Modules:
  0.0 171.1 jit_solution(6481496260545913520)
XLA Ops:
  6.5 0.0 all-gather.4.cloned.1.call-start
  6.5 0.7 slice.13
  7.2 0.8 slice.12
  8.0 3.1 %collective-permute-start = (bf16[16,1536]{1,0:T(8,128)(2,1)S(1)}, bf16[16,1536]{1,0:T(8,128)(2,1)S(1)}, u32[]{:S(2)}, u32[]{:S(2)}) collective-permute-start(bf16[16,1536]{1,0:T(8,128)(2,1)S(1)} %pad_maximum_fusion), channel_id=1, source_target_pairs={{0,4},{4,8},{8,12},{12,16},{16,20},{20,24},{24,28},{1,5},{5,9},{9,... | collective-permute-start | bytes 147464 | tf_op jit(solution)/shard_map/ppermute | solution.py:25
  11.2 1.3 copy.15.a_ref
  12.5 0.7 broadcast_in_dim.35
  13.2 0.7 broadcast_in_dim_reshape.4.d_ref
  13.9 0.0 copy-start.1
  13.9 0.0 copy-start.2
  13.9 0.0 collective-permute-done.before_ref
  13.9 0.0 copy-start
  13.9 0.6 copy-done
  14.5 13.3 %shard_map.118 = (f32[1024,1280]{1,0:T(8,128)}, bf16[1024,128]{1,0:T(8,128)(2,1)}, bf16[64,1024]{1,0:T(8,128)(2,1)}, bf16[128,1280]{1,0:T(8,128)(2,1)}, f32[20,128]{1,0:T(8,128)}) custom-call(bf16[1024,1280]{1,0:T(8,128)(2,1)} %xprev_ref.1, bf16[1024,1280]{1,0:T(8,128)(2,1)} %xprev_ref.1, bf16[1024,256]{1,0:T(8,128)(2,1)} %bcprev_ref.1, ...), custom_call_target="tpu_custom_call" | custom-call | tf_op jit(solution)/shard_map/pallas_call | solution.py:164
  27.9 0.0 all-gather.4.cloned.1.call-update
  27.9 0.0 reduce-scatter.4.cloned.1.call-start
  27.9 0.0 copy-done.1
  27.9 0.6 broadcast_in_dim.40.gain_ref
  28.5 0.0 copy-done.2
  28.5 0.6 dynamic-slice
  29.7 0.8 slice_reduce_fusion
  30.5 0.2 dynamic-update-slice
  30.8 12.7 %all-reduce = f32[160]{0:T(256)S(1)} all-reduce(f32[160]{0:T(256)S(1)} %dynamic-update-slice), channel_id=3, replica_groups=mesh['seq'=8,'head'=4] {'seq'}, use_global_device_ids=true, to_apply=%add | all-reduce | flops 160 | bytes 1280
  43.5 0.1 reshape.8
  43.6 0.1 exponential_select_fusion
  43.7 0.1 broadcast_in_dim.39
  43.8 0.1 mul.18
  43.9 37.6 %all-gather.4.cloned.1.call-done = bf16[1024,1280]{1,0:T(8,128)(2,1)} async-done(((bf16[128,1280]{1,0:T(8,128)(2,1)}), bf16[1024,1280]{1,0:T(8,128)(2,1)}) %all-gather.4.cloned.1.call-update) | async-done | bytes 2621456 | tf_op jit(solution)/shard_map/all_gather | solution.py:213
  81.5 3.1 %fusion.enter_ref = bf16[128,1280]{1,0:T(8,128)(2,1)} fusion(bf16[8,128,1280]{2,1,0:T(8,128)(2,1)} %bitcast.14, f32[8,1280]{1,0:T(8,128)S(1)} %mul.18), kind=kLoop, calls=%fused_computation.1 | loop fusion | flops 3768320 | bytes 2990080 | tf_op jit(solution)/shard_map/reduce_sum | solution.py:218
  84.6 16.5 %shard_map.119 = (bf16[1024,2560]{1,0:T(8,128)(2,1)}, f32[8,1024]{1,0:T(8,128)}) custom-call(f32[1024,1280]{1,0:T(8,128)} %get-tuple-element.12.base_ref, bf16[1024,1280]{1,0:T(8,128)(2,1)} %z_ref.1, bf16[1024,128]{1,0:T(8,128)(2,1)} %get-tuple-element.13.c_ref, bf16[64,1024]{1,0:T(8,128)(2,1)} %get-tuple-element.14.fac2_ref, ...), custom_call_target="tpu_custom_call" | custom-call | tf_op jit(solution)/shard_map/pallas_call | solution.py:220
  101.1 8.0 %copy.16 = bf16[1024,2560]{0,1:T(8,128)(2,1)} copy(bf16[1024,2560]{1,0:T(8,128)(2,1)} %get-tuple-element.17) | data formatting | bytes 10485760
  109.1 0.0 reduce-scatter.4.cloned.1.call-update
  109.1 0.8 slice.15
  109.9 6.4 %psum.7 = f32[1024]{0:T(1024)S(1)} all-reduce(f32[1024]{0:T(1024)S(1)} %bitcast.16), channel_id=1, replica_groups=mesh['seq'=8,'head'=4] {'head'}, use_global_device_ids=true, to_apply=%region_3.4 | all-reduce | flops 1024 | bytes 8192 | tf_op jit(solution)/shard_map/psum | solution.py:239
  116.3 44.9 %reduce-scatter.4.cloned.1.call-done = bf16[640,1024]{1,0:T(8,128)(2,1)} async-done(((bf16[2560,1024]{1,0:T(8,128)(2,1)}), bf16[640,1024]{1,0:T(8,128)(2,1)}) %reduce-scatter.4.cloned.1.call-update) | async-done | bytes 1310736
  161.2 1.7 copy.17
  162.9 1.3 multiply_convert_fusion
  (6 shorter events, 0.1 us)
Async XLA Ops:
  6.5 75.0 %all-gather.4.cloned.1.call-start = ((), (), s32[]{:S(2)}) async-start(), calls=%async_computation.1 | async-start | bytes 2949120 | tf_op jit(solution)/shard_map/all_gather | solution.py:213
  8.0 5.9 %collective-permute-start = (bf16[16,1536]{1,0:T(8,128)(2,1)S(1)}, bf16[16,1536]{1,0:T(8,128)(2,1)S(1)}, u32[]{:S(2)}, u32[]{:S(2)}) collective-permute-start(bf16[16,1536]{1,0:T(8,128)(2,1)S(1)} %pad_maximum_fusion), channel_id=1, source_target_pairs={{0,4},{4,8},{8,12},{12,16},{16,20},{20,24},{24,28},{1,5},{5,9},{9,... | collective-permute-start | bytes 147464 | tf_op jit(solution)/shard_map/ppermute | solution.py:25
  13.9 14.0 %copy-start.1 = (f32[1280]{0:T(1024)S(1)}, f32[1280]{0:T(1024)}, u32[]{:S(2)}) copy-start(f32[1280]{0:T(1024)} %param.20) | copy-start | bytes 15364
  13.9 14.6 %copy-start.2 = (u32[32]{0:T(128)S(1)}, u32[32]{0:T(128)}, u32[]{:S(2)}) copy-start(u32[32]{0:T(128)} %constant.30) | copy-start | bytes 388
  13.9 0.6 copy-start
  27.9 133.3 %reduce-scatter.4.cloned.1.call-start = ((), (), s32[]{:S(2)}) async-start(), calls=%async_computation.2 | async-start | bytes 6553600
Sparse Core Ops, SparseCore 0:
  28.0 53.4 all-gather.3
  109.2 51.9 reduce-scatter.3

commit v2 on v0

v2 whole, which is shorter than its diff:
```python
import functools

import jax
import jax.numpy as jnp
import numpy as np
from jax import lax
from jax.experimental import pallas as pl
from jax.experimental.pallas import tpu as pltpu
from jax.sharding import PartitionSpec as P

P_SIZE = 64
N = 128
Q = 256
CONV = 4
RIM = 16
LANES = 128
CHUNK = 256
SLOT = 32

norm_floor = 0.5


def silu(v):
    return v / (1.0 + jnp.exp(-v))


def dot_t(a, b):
    return lax.dot_general(a, b, (((0,), (0,)), ((), ())), preferred_element_type=jnp.float32)


def conv_rows(padded_ref, taps, cols, rows):
    total = padded_ref[pl.ds(RIM - CONV + 1, rows), cols] * taps[0:1]
    for number in range(1, CONV):
        total = total + padded_ref[pl.ds(RIM - CONV + 1 + number, rows), cols] * taps[number : number + 1]
    return silu(total)


def store_split(ref, at, value, heads):
    high = value.astype(jnp.bfloat16)
    low = (value - high.astype(jnp.float32)).astype(jnp.bfloat16)
    width = value.shape[1]
    ref[0:heads, at : at + width] = high
    ref[SLOT : SLOT + heads, at : at + width] = low


def layer_kernel(
    heads, width, length, depth, channels, shards,
    x_hbm, z_hbm, w_hbm, bc_hbm, bc_ref, dt_ref, a_ref, d_ref, cx_ref, cbc_ref, gain_ref, spread_ref, tri_ref,
    out_ref,
    x_own, z_own, w_own, halo_x, halo_bc, xpad, bcpad, fac, fac2, log_own, log_pair, masked, c_own, bt,
    conv, scaled, run, block_run, state, pair_state, base, chain_out, enter_in, entering, unit,
    sq_out, sq_in, sq_mid, sq_far, one_out, one_in, kept, two_out, two_in,
    local_sem, halo_send, halo_recv, pair_send, pair_recv, chain_send, chain_recv, swap_send, swap_recv,
    one_send, one_recv, two_send, two_recv,
):
    f32, bf16 = jnp.float32, jnp.bfloat16
    blocks = length // Q
    tile = out_ref.shape[1]
    pieces = width // LANES
    half = pieces // 2
    me = lax.axis_index("seq")
    parity = lax.rem(me, 2)
    pair = me // 2
    pairs = shards // 2
    own = lax.axis_index("head")
    near = own + 1 - 2 * lax.rem(own, 2)
    far = lax.rem(own + 2, 4)
    near_far = lax.rem(near + 2, 4)
    mate = me + 1 - 2 * parity

    barrier = pltpu.get_barrier_semaphore()

    def greet(target):
        pl.semaphore_signal(barrier, inc=1, device_id=target, device_id_type=pl.DeviceIdType.MESH)

    loads = [
        pltpu.make_async_copy(x_hbm, x_own, local_sem.at[0]),
        pltpu.make_async_copy(z_hbm, z_own, local_sem.at[1]),
        pltpu.make_async_copy(w_hbm, w_own, local_sem.at[2]),
    ]
    for load in loads:
        load.start()
    for jump in (1, 2):
        @pl.when(me >= jump)
        def _():
            greet({"seq": me - jump})

        @pl.when(me < shards - jump)
        def _():
            greet({"seq": me + jump})
    greet({"head": near})
    greet({"head": far})
    count = 2
    for jump in (1, 2):
        count = count + jnp.where(me >= jump, 1, 0) + jnp.where(me < shards - jump, 1, 0)
    pl.semaphore_wait(barrier, count)

    def remote(source, target, send, recv, device):
        return pltpu.make_async_remote_copy(
            src_ref=source, dst_ref=target, send_sem=send, recv_sem=recv,
            device_id=device, device_id_type=pl.DeviceIdType.MESH,
        )

    after = jnp.minimum(me + 1, shards - 1)
    halo = [
        remote(x_hbm.at[pl.ds(length - RIM, RIM)], halo_x, halo_send.at[0], halo_recv.at[0], {"seq": after}),
        remote(bc_hbm.at[pl.ds(length - RIM, RIM)], halo_bc, halo_send.at[1], halo_recv.at[1], {"seq": after}),
    ]

    @pl.when(me < shards - 1)
    def _():
        for copy in halo:
            copy.start()

    @pl.when(me == 0)
    def _():
        halo_x[...] = jnp.zeros_like(halo_x)
        halo_bc[...] = jnp.zeros_like(halo_bc)

    fac[...] = jnp.zeros_like(fac)
    fac2[...] = jnp.zeros_like(fac2)
    tri = tri_ref[...]
    before_log = jnp.zeros((heads, 1), f32)
    for block in range(blocks):
        dt = dt_ref[:, block * Q : (block + 1) * Q]
        step = jnp.maximum(dt, 0.0) + jnp.log1p(jnp.exp(-jnp.abs(dt)))
        rest = -jnp.exp(a_ref[...]) * step
        cum = jnp.zeros_like(rest)
        for _ in range(3):
            piece = rest.astype(bf16)
            cum = cum + jnp.dot(piece, tri, preferred_element_type=f32)
            rest = rest - piece.astype(f32)
        last = cum[:, Q - 1 : Q]
        mid = 0.5 * last
        here = fac.at[block]
        store_split(here, 0, jnp.exp(cum - mid), heads)
        store_split(here, Q, jnp.exp(mid - cum) * step, heads)
        lane = lax.broadcasted_iota(jnp.int32, (heads, LANES), 1)
        scal = jnp.where(lane == 0, last, jnp.where(lane == 1, mid, last - mid))
        store_split(here, 2 * Q, jnp.exp(scal), heads)
        store_split(fac2.at[block], 0, jnp.exp(before_log + cum), heads)
        before_log = before_log + last
    log_own[...] = jnp.broadcast_to(before_log, log_own.shape)

    def wide_row(logs, cols):
        value = jnp.exp(logs)
        high = value.astype(bf16)
        low = (value - high.astype(f32)).astype(bf16)
        both = dot_t(high, spread_ref[0:heads, cols]) + dot_t(low, spread_ref[0:heads, cols])
        return both[0:1]

    @pl.when(me > 0)
    def _():
        for copy in halo:
            copy.wait_recv()

    loads[0].wait()
    run[...] = jnp.zeros_like(run)

    @pl.loop(0, blocks)
    def _(block):
        start = pl.multiple_of(block * Q, Q)

        @pl.when(block == 0)
        def _():
            xpad[0:RIM, :] = halo_x[...].astype(f32)
            bcpad[0:RIM, :] = halo_bc[...].astype(f32)

        @pl.when(block > 0)
        def _():
            rim = pl.multiple_of(block * Q - RIM, RIM)
            xpad[0:RIM, :] = x_own[pl.ds(rim, RIM), :].astype(f32)
            bcpad[0:RIM, :] = bc_ref[pl.ds(rim, RIM), :].astype(f32)

        xpad[RIM : RIM + Q, :] = x_own[pl.ds(start, Q), :].astype(f32)
        bcpad[RIM : RIM + Q, :] = bc_ref[pl.ds(start, Q), :].astype(f32)
        bc = conv_rows(bcpad, cbc_ref[...], slice(None), Q)
        b_part = bc[:, :N].astype(bf16)
        c_part = bc[:, N:].astype(bf16)
        c_own[pl.ds(start, Q), :] = c_part
        bt[...] = bc[:, :N].T.astype(bf16)
        scores = lax.dot_general(c_part, b_part, (((1,), (1,)), ((), ())), preferred_element_type=f32)
        rows_at = lax.broadcasted_iota(jnp.int32, (Q, Q), 0)
        cols_at = lax.broadcasted_iota(jnp.int32, (Q, Q), 1)
        masked[block] = jnp.where(rows_at >= cols_at, scores, 0.0).astype(bf16)
        for col in range(0, width, CHUNK):
            cols = slice(col, col + CHUNK)
            wide = dot_t(fac[block, :, Q : 2 * Q + LANES], spread_ref[:, cols])
            xc = conv_rows(xpad, cx_ref[:, cols], cols, Q).astype(bf16)
            conv[pl.ds(start, Q), cols] = xc
            now = (xc.astype(f32) * wide[0:Q]).astype(bf16)
            scaled[pl.ds(start, Q), cols] = now
            held = run[:, cols]
            block_run[block, :, cols] = (held * wide[Q + 1 : Q + 2]).astype(bf16)
            added = jnp.dot(bt[...], now, preferred_element_type=f32)
            run[:, cols] = held * wide[Q : Q + 1] + wide[Q + 2 : Q + 3] * added

    for number in range(pieces):
        state[number] = run[:, number * LANES : (number + 1) * LANES].astype(bf16)

    first = parity * half
    other = half - first
    give = [
        remote(log_own, log_pair, pair_send.at[0], pair_recv.at[0], {"seq": mate}),
        remote(state.at[pl.ds(other, half)], pair_state.at[pl.ds(other, half)], pair_send.at[1], pair_recv.at[1], {"seq": mate}),
    ]
    give_rest = remote(state.at[pl.ds(first, half)], pair_state.at[pl.ds(first, half)], pair_send.at[2], pair_recv.at[2], {"seq": mate})
    take = [
        remote(log_own, log_pair, pair_send.at[0], pair_recv.at[0], {"seq": mate}),
        remote(state.at[pl.ds(first, half)], pair_state.at[pl.ds(first, half)], pair_send.at[1], pair_recv.at[1], {"seq": mate}),
    ]
    for copy in give:
        copy.start()

    @pl.when(parity == 0)
    def _():
        give_rest.start()

    def intra(block):
        start = pl.multiple_of(block * Q, Q)
        for col in range(0, width, CHUNK):
            cols = slice(col, col + CHUNK)
            wide = dot_t(fac[block, :, 0:Q], spread_ref[:, cols])
            y = jnp.dot(masked[block], scaled[pl.ds(start, Q), cols], preferred_element_type=f32)
            y = y + jnp.dot(c_own[pl.ds(start, Q), :], block_run[block, :, cols], preferred_element_type=f32)
            base[pl.ds(start, Q), cols] = wide * y + d_ref[:, cols] * conv[pl.ds(start, Q), cols].astype(f32)

    ahead = jnp.minimum(me + 2, shards - 1)

    def chain_copy(k):
        return remote(chain_out.at[k], enter_in.at[first + k], chain_send.at[k], chain_recv.at[k], {"seq": ahead})

    def swap_copy(k, at):
        return remote(enter_in.at[at + k], enter_in.at[at + k], swap_send.at[k], swap_recv.at[k], {"seq": mate})

    def exchange():
        for copy in take:
            copy.wait_recv()
        mine = log_own[...]
        theirs = log_pair[...]
        later = jnp.where(parity == 0, theirs, mine)

        @pl.when(pair == 0)
        def _():
            enter_in[...] = jnp.zeros_like(enter_in)

        for k in range(half):
            @pl.when(pair > 0)
            def _():
                chain_copy(k).wait_recv()
                swap_copy(k, first).start()

            @pl.when(pair < pairs - 1)
            def _():
                rows = jnp.where(parity == 0, wide_row(later, slice(k * LANES, (k + 1) * LANES)),
                                 wide_row(later, slice((half + k) * LANES, (half + k + 1) * LANES)))
                both = jnp.where(parity == 0, wide_row(mine + theirs, slice(k * LANES, (k + 1) * LANES)),
                                 wide_row(mine + theirs, slice((half + k) * LANES, (half + k + 1) * LANES)))
                mine_k = state[first + k].astype(f32)
                theirs_k = pair_state[first + k].astype(f32)
                early = jnp.where(parity == 0, mine_k, theirs_k)
                late = jnp.where(parity == 0, theirs_k, mine_k)
                total = both * enter_in[first + k].astype(f32) + rows * early + late
                chain_out[k] = total.astype(bf16)
                chain_copy(k).start()

    ready = jnp.minimum(pair, blocks)

    @pl.loop(0, blocks + 1)
    def _(turn):
        @pl.when(turn == ready)
        def _():
            exchange()

        @pl.when(turn < blocks)
        def _():
            intra(turn)

    @pl.when(pair > 0)
    def _():
        for k in range(half):
            swap_copy(k, other).wait_recv()

    @pl.when(parity == 1)
    def _():
        give_rest.wait_recv()
        for k in range(pieces):
            row = wide_row(log_pair[...], slice(k * LANES, (k + 1) * LANES))
            value = row * enter_in[k].astype(f32) + pair_state[k].astype(f32)
            entering[:, k * LANES : (k + 1) * LANES] = value.astype(bf16)

    @pl.when(parity == 0)
    def _():
        for k in range(pieces):
            entering[:, k * LANES : (k + 1) * LANES] = enter_in[k]

    loads[1].wait()
    loads[2].wait()

    def near_copies(block):
        return [
            remote(one_out.at[block], one_in.at[block], one_send.at[block, 0], one_recv.at[block, 0], {"head": near}),
            remote(sq_out.at[block], sq_in.at[block], one_send.at[block, 1], one_recv.at[block, 1], {"head": near}),
        ]

    def far_copies(block):
        return [
            remote(two_out.at[block], two_in.at[block], two_send.at[block, 0], two_recv.at[block, 0], {"head": far}),
            remote(sq_mid.at[block], sq_far.at[block], two_send.at[block, 1], two_recv.at[block, 1], {"head": far}),
        ]

    def product(index):
        at = pl.multiple_of(index * tile, LANES)
        return jnp.dot(unit[...], w_own[:, pl.ds(at, tile)], preferred_element_type=f32)

    @pl.loop(0, blocks)
    def _(block):
        start = pl.multiple_of(block * Q, Q)
        rows = pl.ds(start, Q)
        total = jnp.zeros((Q, LANES), f32)
        for col in range(0, width, CHUNK):
            cols = slice(col, col + CHUNK)
            wide = dot_t(fac2[block], spread_ref[:, cols])
            outer = jnp.dot(c_own[rows, :], entering[:, cols], preferred_element_type=f32)
            mixed = base[rows, cols] + wide * outer
            gated = mixed * silu(z_own[rows, cols].astype(f32))
            square = gated * gated
            for part in range(0, CHUNK, LANES):
                total = total + square[:, part : part + LANES]
            unit[:, cols] = (gated * gain_ref[:, cols]).astype(bf16)
        sq_out[block] = lax.dot_general(
            jnp.ones((8, LANES), f32), total, (((1,), (1,)), ((), ())),
            precision=lax.Precision.HIGHEST, preferred_element_type=f32,
        )
        one_out[block, 0] = product(near_far).astype(bf16)
        one_out[block, 1] = product(near).astype(bf16)
        for copy in near_copies(block):
            copy.start()
        two = product(far)
        kept[block] = product(own)
        for copy in near_copies(block):
            copy.wait_recv()
        two_out[block] = (two + one_in[block, 0].astype(f32)).astype(bf16)
        sq_mid[block] = sq_out[block] + sq_in[block]
        for copy in far_copies(block):
            copy.start()
        kept[block] = kept[block] + one_in[block, 1].astype(f32)

    @pl.loop(0, blocks)
    def _(block):
        start = pl.multiple_of(block * Q, Q)
        for copy in far_copies(block):
            copy.wait_recv()
        squares = sq_mid[block] + sq_far[block]
        column = lax.dot_general(
            squares, jnp.full((8, LANES), 0.125, f32), (((0,), (0,)), ((), ())),
            precision=lax.Precision.HIGHEST, preferred_element_type=f32,
        )
        scale = lax.rsqrt(column / channels + norm_floor)[:, 0:1]
        out_ref[pl.ds(start, Q), :] = ((kept[block] + two_in[block].astype(f32)) * scale).astype(bf16)

    @pl.loop(0, blocks)
    def _(block):
        for copy in near_copies(block) + far_copies(block):
            copy.wait_send()

    @pl.when(me < shards - 1)
    def _():
        for copy in halo:
            copy.wait_send()

    for copy in give:
        copy.wait_send()

    @pl.when(parity == 0)
    def _():
        give_rest.wait_send()

    for k in range(half):
        @pl.when(pair > 0)
        def _():
            swap_copy(k, first).wait_send()

        @pl.when(pair < pairs - 1)
        def _():
            chain_copy(k).wait_send()


def local(shards, channels, x_raw, bc_raw, z_gate, dt_raw, a_log, d_skip, conv_x, conv_bc, norm_gain, w_out):
    length, width = x_raw.shape
    heads = a_log.shape[0]
    blocks = length // Q
    depth = w_out.shape[1]
    tile = depth // lax.axis_size("head")
    pieces = width // LANES
    half = pieces // 2
    spread = np.zeros((2 * SLOT, width), np.float32)
    for head in range(heads):
        spread[head, head * P_SIZE : (head + 1) * P_SIZE] = 1.0
        spread[SLOT + head, head * P_SIZE : (head + 1) * P_SIZE] = 1.0
    spread = jnp.asarray(spread, jnp.bfloat16)
    tri = jnp.asarray(np.triu(np.ones((Q, Q), np.float32)), jnp.bfloat16)
    d_wide = jnp.repeat(d_skip, P_SIZE)[None]
    f32, bf16 = jnp.float32, jnp.bfloat16
    anywhere = pl.BlockSpec(memory_space=pl.ANY)
    inside = pl.BlockSpec(memory_space=pltpu.VMEM)
    vmem = pltpu.VMEM
    dma = pltpu.SemaphoreType.DMA
    return pl.pallas_call(
        functools.partial(layer_kernel, heads, width, length, depth, channels, shards),
        in_specs=[anywhere] * 4 + [inside] * 9,
        out_specs=inside,
        out_shape=jax.ShapeDtypeStruct((length, tile), bf16),
        scratch_shapes=[
            vmem((length, width), bf16),
            vmem((length, width), bf16),
            vmem((width, depth), bf16),
            vmem((RIM, width), bf16),
            vmem((RIM, 2 * N), bf16),
            vmem((RIM + Q, width), f32),
            vmem((RIM + Q, 2 * N), f32),
            vmem((blocks, 2 * SLOT, 2 * Q + LANES), bf16),
            vmem((blocks, 2 * SLOT, Q), bf16),
            vmem((heads, LANES), f32),
            vmem((heads, LANES), f32),
            vmem((blocks, Q, Q), bf16),
            vmem((length, N), bf16),
            vmem((N, Q), bf16),
            vmem((length, width), bf16),
            vmem((length, width), bf16),
            vmem((N, width), f32),
            vmem((blocks, N, width), bf16),
            vmem((pieces, N, LANES), bf16),
            vmem((pieces, N, LANES), bf16),
            vmem((length, width), f32),
            vmem((half, N, LANES), bf16),
            vmem((pieces, N, LANES), bf16),
            vmem((N, width), bf16),
            vmem((Q, width), bf16),
            vmem((blocks, 8, Q), f32),
            vmem((blocks, 8, Q), f32),
            vmem((blocks, 8, Q), f32),
            vmem((blocks, 8, Q), f32),
            vmem((blocks, 2, Q, tile), bf16),
            vmem((blocks, 2, Q, tile), bf16),
            vmem((blocks, Q, tile), f32),
            vmem((blocks, Q, tile), bf16),
            vmem((blocks, Q, tile), bf16),
            dma((3,)), dma((2,)), dma((2,)), dma((3,)), dma((3,)),
            dma((half,)), dma((half,)), dma((half,)), dma((half,)),
            dma((blocks, 2)), dma((blocks, 2)), dma((blocks, 2)), dma((blocks, 2)),
        ],
        compiler_params=pltpu.CompilerParams(
            collective_id=0, has_side_effects=True, vmem_limit_bytes=63 << 20
        ),
    )(x_raw, z_gate, w_out, bc_raw, bc_raw, dt_raw, a_log[:, None], d_wide, conv_x, conv_bc, norm_gain[None], spread, tri)


def solution(mesh):
    in_specs = (
        P("seq", "head"),
        P("seq", None),
        P("seq", "head"),
        P("head", "seq"),
        P("head"),
        P("head"),
        P(None, "head"),
        P(),
        P("head"),
        P("head", None),
    )

    def whole(x_raw, *rest):
        body = functools.partial(local, mesh.shape["seq"], x_raw.shape[1])
        return jax.shard_map(
            body, mesh=mesh, in_specs=in_specs, out_specs=P("seq", "head"), check_vma=False
        )(x_raw, *rest)

    return whole
```

time: 208 us -> 77.1 us (0.37); the launches traced: 205 us -> 76.6 us
  waiting for transfers between devices: 70.3 us -> 0 us
  Pallas kernels: 0 us -> 70.1 us
  local copies, waits for them, and re-layouts: 41.2 us -> 6.51 us
  matrix products: 32.8 us -> 0 us
  other arithmetic: 24.8 us -> 0 us
  blocking collectives: 18.5 us -> 0 us
  between operations: 14.5 us -> 0.01 us
  starting transfers between devices: 3.18 us -> 0 us
    pallas_call x0 -> x1, Pallas kernels: none -> 70.1 us  [local(): pl.pallas_call(functools.partial(layer_kernel, heads, width, length, dept...]
    unnamed x3 -> x0, waiting for transfers between devices: 41.4 us -> none
    dot_general x6 -> x0, matrix products: 32.8 us -> none  [the longest x1 9.89 us: local(): jnp.dot(unit, w_out, preferred_element_type=jnp.float32)]
    all_gather x1 -> x0, waiting for transfers between devices: 28.8 us -> none  [local(): lax.all_gather(running[None].astype(jnp.bfloat16), 'seq', axis=0, tiled=T...]
    unnamed x61 -> x1, local copies, waits for them, and re-layouts: 21.4 us -> 2.49 us
    unnamed x1 -> x0, blocking collectives: 12.1 us -> none
    convert_element_type x5 -> x0, other arithmetic: 11.5 us -> none  [the longest x2 8.26 us: conv_with(): return jax.nn.silu(total).astype(jnp.bfloat16)]
    slice x11 -> x0, local copies, waits for them, and re-layouts: 7.47 us -> none  [the longest x2 2.98 us: conv_with(): taps[number][None, :]]
  transfers between devices with their start and end apart: 3 -> 0, of which waited for: 2 -> 0; matrix products, arithmetic and copies ran while one was open for 13% -> 0% of each run, Pallas kernels for 0% -> 0%
where the time goes in v2:
time: 77.1 us; the launch traced here: 76.6 us
  Pallas kernels  70.1 us (91%)
  local copies, waits for them, and re-layouts  6.51 us (8%)
    pallas_call x1, Pallas kernels, local(): pl.pallas_call(functools.partial(layer_kernel, heads, width, length, dept...  70.1 us
    unnamed x1, local copies, waits for them, and re-layouts  2.49 us

profile of v2, /device:TPU:25, one launch (start us, length us, event | category | flops | bytes accessed | tf_op | source)
XLA Modules:
  0.0 76.6 jit_solution(477762363597119229)
XLA Ops:
  0.0 1.3 %broadcast_in_dim.11.gain_ref = f32[1,1280]{1,0:T(1,128)} reshape(f32[1280]{0:T(1024)} %param.20) | data formatting | bytes 10240 | tf_op jit(solution)/shard_map/broadcast_in_dim | solution.py:456
  1.3 1.3 %copy.13.a_ref = f32[20,1]{1,0:T(8,128)} copy(f32[20,1]{0,1:T(1,128)} %bitcast.1) | data formatting | bytes 160 | tf_op jit(solution)/shard_map/broadcast_in_dim | solution.py:456
  2.6 0.7 broadcast_in_dim.10
  3.4 0.7 broadcast_in_dim_reshape.3.d_ref
  4.0 70.1 %shard_map.118 = bf16[1024,640]{1,0:T(8,128)(2,1)} custom-call(bf16[1024,1280]{1,0:T(8,128)(2,1)} %x_hbm.1, bf16[1024,1280]{1,0:T(8,128)(2,1)} %z_hbm.1, bf16[1280,2560]{1,0:T(8,128)(2,1)} %w_hbm.1, bf16[1024,256]{1,0:T(8,128)(2,1)} %bc_ref.1, bf16[1024,256]{1,0:T(8,128)(2,1)} %bc_ref.1, f32[20,1024]{1,0:T(8,128)} %dt_ref.1, f32[20,1]{1,0:T(8,128)} %copy.13.a_ref, ...), custom_call_target="tpu_custom_call" | custom-call | tf_op jit(solution)/shard_map/pallas_call | solution.py:409
  74.1 2.5 %copy.15 = bf16[1024,640]{1,0:T(8,128)(2,1)} copy(bf16[1024,640]{1,0:T(8,128)(2,1)} %shard_map.118) | data formatting | bytes 2621440

commit v3 on v2

v3 whole, which is shorter than its diff:
```python
import functools

import jax
import jax.numpy as jnp
import numpy as np
from jax import lax
from jax.experimental import pallas as pl
from jax.experimental.pallas import tpu as pltpu
from jax.sharding import PartitionSpec as P

P_SIZE = 64
N = 128
Q = 256
CONV = 4
RIM = 16
LANES = 128
CHUNK = 256
SLOT = 32

norm_floor = 0.5


def silu(v):
    return v / (1.0 + jnp.exp(-v))


def dot_t(a, b):
    return lax.dot_general(a, b, (((0,), (0,)), ((), ())), preferred_element_type=jnp.float32)


def conv_rows(padded_ref, taps, at):
    first = RIM - CONV + 1 + at
    total = padded_ref[first : first + Q, :] * taps[0:1]
    for number in range(1, CONV):
        total = total + padded_ref[first + number : first + number + Q, :] * taps[number : number + 1]
    return silu(total)


def store_split(ref, at, value, heads):
    high = value.astype(jnp.bfloat16)
    low = (value - high.astype(jnp.float32)).astype(jnp.bfloat16)
    width = value.shape[1]
    ref[0:heads, at : at + width] = high
    ref[SLOT : SLOT + heads, at : at + width] = low


def layer_kernel(
    heads, width, length, depth, channels, shards,
    x_hbm, z_hbm, w_hbm, bc_hbm, bc_ref, dt_ref, a_ref, d_ref, cx_ref, cbc_ref, gain_ref, spread_ref, tri_ref,
    out_ref,
    x_own, z_own, w_own, halo_x, halo_bc, xpad, bcpad, fac, fac2, log_own, log_pair, masked, c_own, bt,
    conv, scaled, block_run, state, pair_state, row_pair, row_first, pair_total, base, chain_out, enter_in, entering, unit,
    sq_out, sq_in, sq_mid, sq_far, one_out, one_in, kept, two_out, two_in,
    local_sem, halo_send, halo_recv, pair_send, pair_recv, chain_send, chain_recv, swap_send, swap_recv,
    one_send, one_recv, two_send, two_recv, log_sem,
):
    f32, bf16 = jnp.float32, jnp.bfloat16
    blocks = length // Q
    tile = out_ref.shape[1]
    pieces = width // LANES
    half = pieces // 2
    me = lax.axis_index("seq")
    parity = lax.rem(me, 2)
    pair = me // 2
    pairs = shards // 2
    own = lax.axis_index("head")
    near = own + 1 - 2 * lax.rem(own, 2)
    far = lax.rem(own + 2, 4)
    near_far = lax.rem(near + 2, 4)
    mate = me + 1 - 2 * parity

    barrier = pltpu.get_barrier_semaphore()

    def greet(target):
        pl.semaphore_signal(barrier, inc=1, device_id=target, device_id_type=pl.DeviceIdType.MESH)

    loads = [
        pltpu.make_async_copy(x_hbm, x_own, local_sem.at[0]),
        pltpu.make_async_copy(z_hbm, z_own, local_sem.at[1]),
        pltpu.make_async_copy(w_hbm, w_own, local_sem.at[2]),
    ]
    for load in loads:
        load.start()
    for jump in (1, 2):
        @pl.when(me >= jump)
        def _():
            greet({"seq": me - jump})

        @pl.when(me < shards - jump)
        def _():
            greet({"seq": me + jump})
    greet({"head": near})
    greet({"head": far})
    count = 2
    for jump in (1, 2):
        count = count + jnp.where(me >= jump, 1, 0) + jnp.where(me < shards - jump, 1, 0)
    pl.semaphore_wait(barrier, count)

    def remote(source, target, send, recv, device):
        return pltpu.make_async_remote_copy(
            src_ref=source, dst_ref=target, send_sem=send, recv_sem=recv,
            device_id=device, device_id_type=pl.DeviceIdType.MESH,
        )

    after = jnp.minimum(me + 1, shards - 1)
    halo = [
        remote(x_hbm.at[pl.ds(length - RIM, RIM)], halo_x, halo_send.at[0], halo_recv.at[0], {"seq": after}),
        remote(bc_hbm.at[pl.ds(length - RIM, RIM)], halo_bc, halo_send.at[1], halo_recv.at[1], {"seq": after}),
    ]

    @pl.when(me < shards - 1)
    def _():
        for copy in halo:
            copy.start()

    @pl.when(me == 0)
    def _():
        halo_x[...] = jnp.zeros_like(halo_x)
        halo_bc[...] = jnp.zeros_like(halo_bc)

    head_at = lax.broadcasted_iota(jnp.int32, (heads, 1), 0)
    a_col = jnp.zeros((heads, 1), f32)
    d_col = jnp.zeros((heads, 1), f32)
    for head in range(heads):
        a_col = jnp.where(head_at == head, a_ref[head], a_col)
        d_col = jnp.where(head_at == head, d_ref[head], d_col)
    minus_a = -jnp.exp(a_col)
    fac[...] = jnp.zeros_like(fac)
    fac2[...] = jnp.zeros_like(fac2)
    tri = tri_ref[...]
    before_log = jnp.zeros((heads, 1), f32)
    for block in range(blocks):
        dt = dt_ref[:, block * Q : (block + 1) * Q]
        step = jnp.maximum(dt, 0.0) + jnp.log1p(jnp.exp(-jnp.abs(dt)))
        rest = minus_a * step
        cum = jnp.zeros_like(rest)
        for _ in range(3):
            piece = rest.astype(bf16)
            cum = cum + jnp.dot(piece, tri, preferred_element_type=f32)
            rest = rest - piece.astype(f32)
        last = cum[:, Q - 1 : Q]
        mid = 0.5 * last
        here = fac.at[block]
        store_split(here, 0, jnp.exp(cum - mid), heads)
        store_split(here, Q, jnp.exp(mid - cum) * step, heads)
        lane = lax.broadcasted_iota(jnp.int32, (heads, LANES), 1)
        scal = jnp.where(lane == 0, last, jnp.where(lane == 1, mid, last - mid))
        store_split(here, 2 * Q, jnp.exp(scal), heads)
        store_split(fac2.at[block], 0, jnp.exp(before_log + cum), heads)
        before_log = before_log + last
    log_own[...] = jnp.broadcast_to(before_log, log_own.shape)
    give_log = remote(log_own, log_pair, log_sem.at[0], log_sem.at[1], {"seq": mate})
    give_log.start()

    def wide_row(value, cols):
        high = value.astype(bf16)
        low = (value - high.astype(f32)).astype(bf16)
        both = dot_t(high, spread_ref[0:heads, cols]) + dot_t(low, spread_ref[0:heads, cols])
        return both[0:1]

    @pl.when(me > 0)
    def _():
        for copy in halo:
            copy.wait_recv()

    bcpad[0:RIM, :] = halo_bc[...].astype(f32)
    bcpad[RIM : RIM + length, :] = bc_ref[...].astype(f32)
    for block in range(blocks):
        rows = slice(block * Q, (block + 1) * Q)
        bc = conv_rows(bcpad, cbc_ref[...], block * Q)
        c_own[rows, :] = bc[:, N:].astype(bf16)
        bt[:, rows] = bc[:, :N].T.astype(bf16)
    d_wide = wide_row(jnp.broadcast_to(d_col, (heads, LANES)), slice(0, width))
    loads[0].wait()

    first = parity * half
    other = half - first

    def state_copy(index):
        return remote(state.at[index], pair_state.at[index], pair_send.at[index], pair_recv.at[index], {"seq": mate})

    @pl.loop(0, pieces)
    def _(number):
        index = lax.rem(other + number, pieces)
        cols = pl.ds(pl.multiple_of(index * LANES, LANES), LANES)
        xpad[0:RIM, :] = halo_x[:, cols].astype(f32)
        xpad[RIM : RIM + length, :] = x_own[:, cols].astype(f32)
        taps = cx_ref[:, cols]
        held = jnp.zeros((N, LANES), f32)
        for block in range(blocks):
            rows = slice(block * Q, (block + 1) * Q)
            wide = dot_t(fac[block, :, Q : 2 * Q + LANES], spread_ref[:, cols])
            xc = conv_rows(xpad, taps, block * Q).astype(bf16)
            conv[rows, cols] = xc
            now = (xc.astype(f32) * wide[0:Q]).astype(bf16)
            scaled[rows, cols] = now
            block_run[block, index] = (held * wide[Q + 1 : Q + 2]).astype(bf16)
            added = jnp.dot(bt[:, rows], now, preferred_element_type=f32)
            held = held * wide[Q : Q + 1] + wide[Q + 2 : Q + 3] * added
        state[index] = held.astype(bf16)

        @pl.when((number < half) | (parity == 0))
        def _():
            state_copy(index).start()

    def intra(block):
        start = pl.multiple_of(block * Q, Q)
        rows = pl.ds(start, Q)
        c_part = c_own[rows, :]
        scores = jnp.dot(c_part, bt[:, rows], preferred_element_type=f32)
        rows_at = lax.broadcasted_iota(jnp.int32, (Q, Q), 0)
        cols_at = lax.broadcasted_iota(jnp.int32, (Q, Q), 1)
        masked[...] = jnp.where(rows_at >= cols_at, scores, 0.0).astype(bf16)
        for col in range(0, width, CHUNK):
            cols = slice(col, col + CHUNK)
            wide = dot_t(fac[block, :, 0:Q], spread_ref[:, cols])
            y = jnp.dot(masked[...], scaled[rows, cols], preferred_element_type=f32)
            at = col // LANES
            held = jnp.concatenate([block_run[block, at], block_run[block, at + 1]], axis=1)
            y = y + jnp.dot(c_part, held, preferred_element_type=f32)
            base[rows, cols] = wide * y + d_wide[:, cols] * conv[rows, cols].astype(f32)

    ahead = jnp.minimum(me + 2, shards - 1)

    def chain_copy(k):
        return remote(chain_out.at[k], enter_in.at[first + k], chain_send.at[k], chain_recv.at[k], {"seq": ahead})

    def swap_copy(k, at):
        return remote(enter_in.at[at + k], enter_in.at[at + k], swap_send.at[k], swap_recv.at[k], {"seq": mate})

    give_log.wait_recv()
    mine = log_own[...]
    theirs = log_pair[...]
    row_of_pair = jnp.exp(mine + theirs)
    row_of_late = jnp.exp(jnp.where(parity == 0, theirs, mine))
    row_of_early = jnp.exp(theirs)

    @pl.loop(0, half)
    def _(k):
        cols = pl.ds(pl.multiple_of((first + k) * LANES, LANES), LANES)
        state_copy(first + k).wait_recv()
        row_pair[k] = jnp.broadcast_to(wide_row(row_of_pair, cols), (8, LANES))
        mine_k = state[first + k].astype(f32)
        theirs_k = pair_state[first + k].astype(f32)
        early = jnp.where(parity == 0, mine_k, theirs_k)
        late = jnp.where(parity == 0, theirs_k, mine_k)
        pair_total[k] = wide_row(row_of_late, cols) * early + late

    @pl.when(pair == 0)
    def _():
        enter_in[...] = jnp.zeros_like(enter_in)

    def exchange():
        @pl.loop(0, half)
        def _(k):
            @pl.when(pair > 0)
            def _():
                chain_copy(k).wait_recv()

            @pl.when(pair < pairs - 1)
            def _():
                total = row_pair[k, 0:1] * enter_in[first + k].astype(f32) + pair_total[k]
                chain_out[k] = total.astype(bf16)
                chain_copy(k).start()

            @pl.when(pair > 0)
            def _():
                swap_copy(k, first).start()

        @pl.when(parity == 1)
        def _():
            for k in range(pieces):
                row = wide_row(row_of_early, slice(k * LANES, (k + 1) * LANES))
                row_first[k] = jnp.broadcast_to(row, (8, LANES))

    ready = jnp.minimum(pair, blocks)

    @pl.loop(0, blocks + 1)
    def _(turn):
        @pl.when(turn == ready)
        def _():
            exchange()

        @pl.when(turn < blocks)
        def _():
            intra(turn)

    @pl.when(pair > 0)
    def _():
        for k in range(half):
            swap_copy(k, other).wait_recv()

    @pl.when(parity == 1)
    def _():
        for k in range(half):
            state_copy(other + k).wait_recv()
        for k in range(pieces):
            value = row_first[k, 0:1] * enter_in[k].astype(f32) + pair_state[k].astype(f32)
            entering[:, k * LANES : (k + 1) * LANES] = value.astype(bf16)

    @pl.when(parity == 0)
    def _():
        for k in range(pieces):
            entering[:, k * LANES : (k + 1) * LANES] = enter_in[k]

    gain = gain_ref[...].reshape(1, width)
    loads[1].wait()
    loads[2].wait()

    def near_copies(block):
        return [
            remote(one_out.at[block, 0], one_in.at[block, 0], one_send.at[block, 0], one_recv.at[block, 0], {"head": near}),
            remote(sq_out.at[block], sq_in.at[block], one_send.at[block, 1], one_recv.at[block, 1], {"head": near}),
            remote(one_out.at[block, 1], one_in.at[block, 1], one_send.at[block, 2], one_recv.at[block, 2], {"head": near}),
        ]

    def far_copies(block):
        return [
            remote(two_out.at[block], two_in.at[block], two_send.at[block, 0], two_recv.at[block, 0], {"head": far}),
            remote(sq_mid.at[block], sq_far.at[block], two_send.at[block, 1], two_recv.at[block, 1], {"head": far}),
        ]

    def product(index):
        at = pl.multiple_of(index * tile, LANES)
        return jnp.dot(unit[...], w_own[:, pl.ds(at, tile)], preferred_element_type=f32)

    @pl.loop(0, blocks)
    def _(block):
        start = pl.multiple_of(block * Q, Q)
        rows = pl.ds(start, Q)
        total = jnp.zeros((Q, LANES), f32)
        for col in range(0, width, CHUNK):
            cols = slice(col, col + CHUNK)
            wide = dot_t(fac2[block], spread_ref[:, cols])
            outer = jnp.dot(c_own[rows, :], entering[:, cols], preferred_element_type=f32)
            mixed = base[rows, cols] + wide * outer
            gated = mixed * silu(z_own[rows, cols].astype(f32))
            square = gated * gated
            for part in range(0, CHUNK, LANES):
                total = total + square[:, part : part + LANES]
            unit[:, cols] = (gated * gain[:, cols]).astype(bf16)
        sq_out[block] = lax.dot_general(
            jnp.ones((8, LANES), f32), total, (((1,), (1,)), ((), ())),
            precision=lax.Precision.HIGHEST, preferred_element_type=f32,
        )
        copies = near_copies(block)
        one_out[block, 0] = product(near_far).astype(bf16)
        copies[0].start()
        copies[1].start()
        two = product(far)
        copies[0].wait_recv()
        two_out[block] = (two + one_in[block, 0].astype(f32)).astype(bf16)
        copies[1].wait_recv()
        sq_mid[block] = sq_out[block] + sq_in[block]
        for copy in far_copies(block):
            copy.start()
        one_out[block, 1] = product(near).astype(bf16)
        copies[2].start()
        kept[block] = product(own)

    @pl.loop(0, blocks)
    def _(block):
        start = pl.multiple_of(block * Q, Q)
        near_copies(block)[2].wait_recv()
        for copy in far_copies(block):
            copy.wait_recv()
        squares = sq_mid[block] + sq_far[block]
        column = lax.dot_general(
            squares, jnp.full((8, LANES), 0.125, f32), (((0,), (0,)), ((), ())),
            precision=lax.Precision.HIGHEST, preferred_element_type=f32,
        )
        scale = lax.rsqrt(column / channels + norm_floor)[:, 0:1]
        out_ref[pl.ds(start, Q), :] = ((kept[block] + one_in[block, 1].astype(f32) + two_in[block].astype(f32)) * scale).astype(bf16)

    @pl.loop(0, blocks)
    def _(block):
        for copy in near_copies(block) + far_copies(block):
            copy.wait_send()

    @pl.when(me < shards - 1)
    def _():
        for copy in halo:
            copy.wait_send()

    give_log.wait_send()
    for k in range(half):
        state_copy(other + k).wait_send()

        @pl.when(parity == 0)
        def _():
            state_copy(first + k).wait_send()

    for k in range(half):
        @pl.when(pair > 0)
        def _():
            swap_copy(k, first).wait_send()

        @pl.when(pair < pairs - 1)
        def _():
            chain_copy(k).wait_send()


def local(shards, channels, x_raw, bc_raw, z_gate, dt_raw, a_log, d_skip, conv_x, conv_bc, norm_gain, w_out):
    length, width = x_raw.shape
    heads = a_log.shape[0]
    blocks = length // Q
    depth = w_out.shape[1]
    tile = depth // lax.axis_size("head")
    pieces = width // LANES
    half = pieces // 2
    spread = np.zeros((2 * SLOT, width), np.float32)
    for head in range(heads):
        spread[head, head * P_SIZE : (head + 1) * P_SIZE] = 1.0
        spread[SLOT + head, head * P_SIZE : (head + 1) * P_SIZE] = 1.0
    spread = jnp.asarray(spread, jnp.bfloat16)
    tri = jnp.asarray(np.triu(np.ones((Q, Q), np.float32)), jnp.bfloat16)
    f32, bf16 = jnp.float32, jnp.bfloat16
    anywhere = pl.BlockSpec(memory_space=pl.ANY)
    inside = pl.BlockSpec(memory_space=pltpu.VMEM)
    scalars = pl.BlockSpec(memory_space=pltpu.SMEM)
    vmem = pltpu.VMEM
    dma = pltpu.SemaphoreType.DMA
    return pl.pallas_call(
        functools.partial(layer_kernel, heads, width, length, depth, channels, shards),
        in_specs=[anywhere] * 4 + [inside] * 2 + [scalars] * 2 + [inside] * 5,
        out_specs=inside,
        out_shape=jax.ShapeDtypeStruct((length, tile), bf16),
        scratch_shapes=[
            vmem((length, width), bf16),
            vmem((length, width), bf16),
            vmem((width, depth), bf16),
            vmem((RIM, width), bf16),
            vmem((RIM, 2 * N), bf16),
            vmem((RIM + length, LANES), f32),
            vmem((RIM + length, 2 * N), f32),
            vmem((blocks, 2 * SLOT, 2 * Q + LANES), bf16),
            vmem((blocks, 2 * SLOT, Q), bf16),
            vmem((heads, LANES), f32),
            vmem((heads, LANES), f32),
            vmem((Q, Q), bf16),
            vmem((length, N), bf16),
            vmem((N, length), bf16),
            vmem((length, width), bf16),
            vmem((length, width), bf16),
            vmem((blocks, pieces, N, LANES), bf16),
            vmem((pieces, N, LANES), bf16),
            vmem((pieces, N, LANES), bf16),
            vmem((half, 8, LANES), f32),
            vmem((pieces, 8, LANES), f32),
            vmem((half, N, LANES), f32),
            vmem((length, width), f32),
            vmem((half, N, LANES), bf16),
            vmem((pieces, N, LANES), bf16),
            vmem((N, width), bf16),
            vmem((Q, width), bf16),
            vmem((blocks, 8, Q), f32),
            vmem((blocks, 8, Q), f32),
            vmem((blocks, 8, Q), f32),
            vmem((blocks, 8, Q), f32),
            vmem((blocks, 2, Q, tile), bf16),
            vmem((blocks, 2, Q, tile), bf16),
            vmem((blocks, Q, tile), f32),
            vmem((blocks, Q, tile), bf16),
            vmem((blocks, Q, tile), bf16),
            dma((3,)), dma((2,)), dma((2,)), dma((pieces,)), dma((pieces,)),
            dma((half,)), dma((half,)), dma((half,)), dma((half,)),
            dma((blocks, 3)), dma((blocks, 3)), dma((blocks, 2)), dma((blocks, 2)), dma((2,)),
        ],
        compiler_params=pltpu.CompilerParams(
            collective_id=0, has_side_effects=True, vmem_limit_bytes=63 << 20
        ),
    )(x_raw, z_gate, w_out, bc_raw, bc_raw, dt_raw, a_log, d_skip, conv_x, conv_bc, norm_gain, spread, tri)


def solution(mesh):
    in_specs = (
        P("seq", "head"),
        P("seq", None),
        P("seq", "head"),
        P("head", "seq"),
        P("head"),
        P("head"),
        P(None, "head"),
        P(),
        P("head"),
        P("head", None),
    )

    def whole(x_raw, *rest):
        body = functools.partial(local, mesh.shape["seq"], x_raw.shape[1])
        return jax.shard_map(
            body, mesh=mesh, in_specs=in_specs, out_specs=P("seq", "head"), check_vma=False
        )(x_raw, *rest)

    return whole
```

time: 77.1 us -> 68.9 us (0.89)
  local copies, waits for them, and re-layouts: 6.51 us -> 2.49 us
  Pallas kernels: 70.1 us -> 66.2 us
    pallas_call x1, Pallas kernels: 70.1 us -> 66.2 us  [local(): pl.pallas_call(functools.partial(layer_kernel, heads, width, length, dept...]
    broadcast_in_dim x3 -> x0, local copies, waits for them, and re-layouts: 3.35 us -> none  [the longest x1 1.34 us: local(): a_log[:, None]]
where the time goes in v3:
time: 68.9 us; the launch traced here: 68.7 us
  Pallas kernels  66.2 us (96%)
  local copies, waits for them, and re-layouts  2.49 us (4%)
    pallas_call x1, Pallas kernels, local(): pl.pallas_call(functools.partial(layer_kernel, heads, width, length, dept...  66.2 us
    unnamed x1, local copies, waits for them, and re-layouts  2.49 us

profile of v3, /device:TPU:25, one launch (start us, length us, event | category | flops | bytes accessed | tf_op | source)
XLA Modules:
  0.0 68.7 jit_solution(555430518550844913)
XLA Ops:
  0.0 66.2 %shard_map.118 = bf16[1024,640]{1,0:T(8,128)(2,1)} custom-call(bf16[1024,1280]{1,0:T(8,128)(2,1)} %x_hbm.1, bf16[1024,1280]{1,0:T(8,128)(2,1)} %z_hbm.1, bf16[1280,2560]{1,0:T(8,128)(2,1)} %w_hbm.1, bf16[1024,256]{1,0:T(8,128)(2,1)} %bc_ref.1, bf16[1024,256]{1,0:T(8,128)(2,1)} %bc_ref.1, f32[20,1024]{1,0:T(8,128)} %dt_ref.1, f32[20]{0:T(128)} %a_ref.1, ...), custom_call_target="tpu_custom_call" | custom-call | tf_op jit(solution)/shard_map/pallas_call | solution.py:423
  66.2 2.5 %copy.14 = bf16[1024,640]{1,0:T(8,128)(2,1)} copy(bf16[1024,640]{1,0:T(8,128)(2,1)} %shard_map.118) | data formatting | bytes 2621440

commit v4 on v3

--- a/solution.py
+++ b/solution.py
@@ -21,7 +21,8 @@
 
 
 def silu(v):
-    return v / (1.0 + jnp.exp(-v))
+    part = 0.5 * v
+    return part + part * jnp.tanh(part)
 
 
 def dot_t(a, b):
@@ -250,7 +251,17 @@
     def _():
         enter_in[...] = jnp.zeros_like(enter_in)
 
+    def early_rows():
+        for col in range(0, width, CHUNK):
+            row = wide_row(row_of_early, slice(col, col + CHUNK))
+            for at in range(0, CHUNK, LANES):
+                row_first[(col + at) // LANES] = jnp.broadcast_to(row[:, at : at + LANES], (8, LANES))
+
     def exchange():
+        @pl.when((parity == 1) & (pair == pairs - 1))
+        def _():
+            early_rows()
+
         @pl.loop(0, half)
         def _(k):
             @pl.when(pair > 0)
@@ -267,13 +278,11 @@
             def _():
                 swap_copy(k, first).start()
 
-        @pl.when(parity == 1)
-        def _():
-            for k in range(pieces):
-                row = wide_row(row_of_early, slice(k * LANES, (k + 1) * LANES))
-                row_first[k] = jnp.broadcast_to(row, (8, LANES))
-
-    ready = jnp.minimum(pair, blocks)
+        @pl.when((parity == 1) & (pair < pairs - 1))
+        def _():
+            early_rows()
+
+    ready = jnp.where(pair == pairs - 1, blocks, jnp.minimum(pair, blocks - 1))
 
     @pl.loop(0, blocks + 1)
     def _(turn):

time: 68.9 us -> 68.9 us (level)
  no operation moved by 1% of the time
where the time goes in v4:
time: 68.9 us; the launch traced here: 68.7 us
  Pallas kernels  66.3 us (96%)
  local copies, waits for them, and re-layouts  2.49 us (4%)
    pallas_call x1, Pallas kernels, local(): pl.pallas_call(functools.partial(layer_kernel, heads, width, length, dept...  66.3 us
    unnamed x1, local copies, waits for them, and re-layouts  2.49 us

profile of v4, /device:TPU:25, one launch (start us, length us, event | category | flops | bytes accessed | tf_op | source)
XLA Modules:
  0.0 68.7 jit_solution(839097296274419517)
XLA Ops:
  0.0 66.3 %shard_map.118 = bf16[1024,640]{1,0:T(8,128)(2,1)} custom-call(bf16[1024,1280]{1,0:T(8,128)(2,1)} %x_hbm.1, bf16[1024,1280]{1,0:T(8,128)(2,1)} %z_hbm.1, bf16[1280,2560]{1,0:T(8,128)(2,1)} %w_hbm.1, bf16[1024,256]{1,0:T(8,128)(2,1)} %bc_ref.1, bf16[1024,256]{1,0:T(8,128)(2,1)} %bc_ref.1, f32[20,1024]{1,0:T(8,128)} %dt_ref.1, f32[20]{0:T(128)} %a_ref.1, ...), custom_call_target="tpu_custom_call" | custom-call | tf_op jit(solution)/shard_map/pallas_call | solution.py:432
  66.3 2.5 %copy.14 = bf16[1024,640]{1,0:T(8,128)(2,1)} copy(bf16[1024,640]{1,0:T(8,128)(2,1)} %shard_map.118) | data formatting | bytes 2621440
